TPU v7x, 32 devices: a whole 2x2x4 slice. The times are simulated.
32 devices in a mesh: dp: 8 (over y, x, core), tensor: 4 (over z).
Axes of the slice: x: 2, y: 2, z: 4, core: 2. Of those that a mesh axis runs over, the one named last changes fastest.
Arguments:
- tokens: bfloat16 [8192, 1024], P(('dp', 'tensor')), may hold values from -6 to 6
- segments: int32 [8, 1024], P('dp'), may hold values from 0 to 3, never falling along the last dimension, each value on 1 to 512 neighbouring positions
- w_qkv: bfloat16 [1024, 3, 1024], P(None, None, 'tensor'), may hold values from -0.25 to 0.25
- w_out: bfloat16 [1024, 1024], P('tensor'), may hold values from -1 to 1
- w_up: bfloat16 [1024, 4096], P(None, 'tensor'), may hold values from -0.1875 to 0.1875
- w_down: bfloat16 [4096, 1024], P('tensor'), may hold values from -0.09375 to 0.09375
- gain_one: float32 [1024], replicated, may hold values from 0.5 to 1.5
- shift_one: float32 [1024], replicated, may hold values from -2 to 2
- gain_two: float32 [1024], replicated, may hold values from 0.5 to 1.5
- shift_two: float32 [1024], replicated, may hold values from -2 to 2
- cotangent: bfloat16 [8192, 1024], P(('dp', 'tensor')), may hold values from -6 to 6
Outputs:
- output_rows: bfloat16 [8192, 1024], P(('dp', 'tensor'))
- input_grad: bfloat16 [8192, 1024], P(('dp', 'tensor'))
- grad_qkv: float32 [1024, 3, 1024], P(None, None, 'tensor')
- grad_out: float32 [1024, 1024], P('tensor')
- grad_up: float32 [1024, 4096], P(None, 'tensor')
- grad_down: float32 [4096, 1024], P('tensor')
- grad_gain_one: float32 [1024], replicated
- grad_shift_one: float32 [1024], replicated
- grad_gain_two: float32 [1024], replicated
- grad_shift_two: float32 [1024], replicated
- rms_context: float32 [], replicated
- rms_active: float32 [], replicated
Inputs may be any that keep to these rules, and one draw needn't show every extreme that they name: `segments`: within a row (one data group), sequence numbers start at 0, never fall and step by one; each sequence holds 1 to 512 tokens and one holds exactly 512.
All inputs are finite; a program needn't handle non-finite values.
Results may differ from a plain program's by a relative error of at most 0.006.
The roundings to bfloat16 on the way count: a program that leaves them out, or rounds other values in their place, can miss the bound.
Values may be sent and summed in bfloat16 or wider, within the bound.
A program may use at most 128 MiB of HBM per device.

v0:
```python
from functools import partial

import jax
import jax.numpy as jnp
from jax import lax
from jax.sharding import PartitionSpec as P

HS = 64
ROT = 16
FF = 4096
QBLK = 512


epsilon = 1e-05
rotary_base = 10000.0
masked_score = -1000000000.0


def layer_norm(values, gain_vector, shift_vector):
    average = jnp.mean(values, axis=-1, keepdims=True)
    centred = values - average
    variance = jnp.mean(centred * centred, axis=-1, keepdims=True)
    return centred * lax.rsqrt(variance + epsilon) * gain_vector + shift_vector


def exact_gelu(values):
    return jax.nn.gelu(values, approximate=False)


def seq_positions(seg_row):
    row_index = jnp.arange(seg_row.shape[0], dtype=jnp.int32)
    starts_here = jnp.concatenate([jnp.ones((1,), dtype=bool), seg_row[1:] != seg_row[:-1]])
    seq_start = lax.cummax(jnp.where(starts_here, row_index, 0), axis=0)
    return row_index - seq_start


def rotary_angles(seg_row):
    half_rot = ROT // 2
    frequency = rotary_base ** (-(2.0 * jnp.arange(half_rot, dtype=jnp.float32)) / ROT)
    return seq_positions(seg_row).astype(jnp.float32)[:, None] * frequency[None, :]


def rotate(vectors, angles):
    half_rot = ROT // 2
    shape_rot = (angles.shape[0],) + (1,) * (vectors.ndim - 2) + (half_rot,)
    cosine = jnp.cos(angles).reshape(shape_rot)
    sine_part = jnp.sin(angles).reshape(shape_rot)
    front = vectors[..., :half_rot]
    behind = vectors[..., half_rot:ROT]
    return jnp.concatenate(
        [
            front * cosine - behind * sine_part,
            behind * cosine + front * sine_part,
            vectors[..., ROT:],
        ],
        axis=-1,
    )


def masked_scores(block_queries, keys_all, seg_row, start):
    query_index = start + jnp.arange(QBLK, dtype=jnp.int32)
    key_index = jnp.arange(seg_row.shape[0], dtype=jnp.int32)
    seg_block = lax.dynamic_slice_in_dim(seg_row, start, QBLK, 0)
    allowed = (seg_block[:, None] == seg_row[None, :]) & (
        key_index[None, :] <= query_index[:, None]
    )
    scores = jnp.einsum(
        "qhd,khd->hqk", block_queries, keys_all, preferred_element_type=jnp.float32
    ) * HS ** (-0.5)
    return jnp.where(allowed[None], scores, masked_score)


def per_device(
    tokens,
    segments,
    w_qkv,
    w_out,
    w_up,
    w_down,
    gain_one,
    shift_one,
    gain_two,
    shift_two,
    cotangent,
):
    seg_row = segments[0]
    group = seg_row.shape[0]
    width = tokens.shape[1]
    local_width = w_qkv.shape[2]
    heads_local = local_width // HS
    block_starts = jnp.arange(group // QBLK, dtype=jnp.int32) * QBLK
    tokens_own = tokens.astype(jnp.float32)
    cotangent_own = cotangent.astype(jnp.float32)
    normed_full_one, back_one = jax.vjp(layer_norm, tokens_own, gain_one, shift_one)
    normed_full_two, back_two = jax.vjp(layer_norm, tokens_own, gain_two, shift_two)
    normed_one, normed_two = (
        lax.all_gather(normed_full_one.astype(jnp.bfloat16), "tensor", axis=0, tiled=True),
        lax.all_gather(normed_full_two.astype(jnp.bfloat16), "tensor", axis=0, tiled=True),
    )
    qkv_matrix = w_qkv.reshape(width, 3 * local_width)
    projected = jnp.dot(normed_one, qkv_matrix, preferred_element_type=jnp.float32).reshape(
        group, 3, heads_local, HS
    )
    angles = rotary_angles(seg_row)
    turned = rotate(projected[:, 0:2], angles).astype(jnp.bfloat16)
    queries = turned[:, 0]
    keys_all = turned[:, 1]
    values_all = projected[:, 2].astype(jnp.bfloat16)

    def forward_block(start):
        block_queries = lax.dynamic_slice_in_dim(queries, start, QBLK, 0)
        scores = masked_scores(block_queries, keys_all, seg_row, start)
        row_max = jnp.max(scores, axis=-1, keepdims=True)
        weights_exp = jnp.exp(scores - row_max)
        total_exp = jnp.sum(weights_exp, axis=-1, keepdims=True)
        weights_soft = (weights_exp / total_exp).astype(jnp.bfloat16)
        block_context = jnp.einsum(
            "hqk,khd->qhd", weights_soft, values_all, preferred_element_type=jnp.float32
        )
        return (block_context, (row_max + jnp.log(total_exp))[..., 0])

    context_blocks, log_totals = lax.map(forward_block, block_starts)
    context = context_blocks.reshape(group, local_width)
    square_context = jnp.sum(context * context)
    context_low = context.astype(jnp.bfloat16)
    hidden = jnp.dot(normed_two, w_up, preferred_element_type=jnp.float32)
    activated, gelu_back = jax.vjp(exact_gelu, hidden)
    square_active = jnp.sum(activated * activated)
    active_low = activated.astype(jnp.bfloat16)
    partial_rows = jnp.dot(context_low, w_out, preferred_element_type=jnp.float32) + jnp.dot(
        active_low, w_down, preferred_element_type=jnp.float32
    )
    branch = lax.psum_scatter(partial_rows, "tensor", scatter_dimension=0, tiled=True)
    output_rows = (tokens_own + branch).astype(jnp.bfloat16)
    cotangent_all = lax.all_gather(cotangent, "tensor", axis=0, tiled=True)
    grad_down = jnp.einsum(
        "tf,td->fd", active_low, cotangent_all, preferred_element_type=jnp.float32
    )
    grad_active = jnp.einsum("td,fd->tf", cotangent_all, w_down, preferred_element_type=jnp.float32)
    grad_hidden = gelu_back(grad_active)[0].astype(jnp.bfloat16)
    grad_up = jnp.einsum("td,tf->df", normed_two, grad_hidden, preferred_element_type=jnp.float32)
    grad_normed_two = jnp.einsum("tf,df->td", grad_hidden, w_up, preferred_element_type=jnp.float32)
    grad_out = jnp.einsum(
        "tc,td->cd", context_low, cotangent_all, preferred_element_type=jnp.float32
    )
    grad_context = (
        jnp.einsum("td,cd->tc", cotangent_all, w_out, preferred_element_type=jnp.float32)
        .astype(jnp.bfloat16)
        .reshape(group, heads_local, HS)
    )
    score_scale = HS ** (-0.5)

    def backward_block(running, item):
        start, log_total = item
        grad_keys, grad_values = running
        block_queries = lax.dynamic_slice_in_dim(queries, start, QBLK, 0)
        block_grad = lax.dynamic_slice_in_dim(grad_context, start, QBLK, 0)
        scores = masked_scores(block_queries, keys_all, seg_row, start)
        weights_soft = jnp.exp(scores - log_total[..., None])
        weights_low = weights_soft.astype(jnp.bfloat16)
        grad_values = grad_values + jnp.einsum(
            "hqk,qhd->khd", weights_low, block_grad, preferred_element_type=jnp.float32
        )
        grad_weights = jnp.einsum(
            "qhd,khd->hqk", block_grad, values_all, preferred_element_type=jnp.float32
        )
        inner_sum = jnp.sum(weights_soft * grad_weights, axis=-1, keepdims=True)
        grad_scores = (weights_soft * (grad_weights - inner_sum)).astype(jnp.bfloat16)
        grad_block_queries = (
            jnp.einsum("hqk,khd->qhd", grad_scores, keys_all, preferred_element_type=jnp.float32)
            * score_scale
        )
        grad_keys = (
            grad_keys
            + jnp.einsum(
                "hqk,qhd->khd", grad_scores, block_queries, preferred_element_type=jnp.float32
            )
            * score_scale
        )
        return ((grad_keys, grad_values), grad_block_queries)

    zero_heads = jnp.zeros((group, heads_local, HS), jnp.float32)
    (grad_keys, grad_values), grad_query_blocks = lax.scan(
        backward_block, (zero_heads, zero_heads), (block_starts, log_totals)
    )
    grad_queries = grad_query_blocks.reshape(group, heads_local, HS)
    _, rotate_back = jax.vjp(partial(rotate, angles=angles), projected[:, 0:2])
    grad_turned = rotate_back(jnp.stack([grad_queries, grad_keys], axis=1))[0]
    grad_projected = (
        jnp.concatenate([grad_turned, grad_values[:, None]], axis=1)
        .astype(jnp.bfloat16)
        .reshape(group, 3 * local_width)
    )
    grad_qkv = jnp.einsum(
        "td,tc->dc", normed_one, grad_projected, preferred_element_type=jnp.float32
    ).reshape(width, 3, local_width)
    grad_normed_one = jnp.einsum(
        "tc,dc->td", grad_projected, qkv_matrix, preferred_element_type=jnp.float32
    )
    grad_qkv, grad_out, grad_up, grad_down = lax.psum(
        (grad_qkv, grad_out, grad_up, grad_down), "dp"
    )
    grad_shard_one, grad_shard_two = (
        lax.psum_scatter(grad_normed_one, "tensor", scatter_dimension=0, tiled=True),
        lax.psum_scatter(grad_normed_two, "tensor", scatter_dimension=0, tiled=True),
    )
    grad_rows_one, grad_gain_one, grad_shift_one = back_one(grad_shard_one)
    grad_rows_two, grad_gain_two, grad_shift_two = back_two(grad_shard_two)
    grad_input_rows = grad_rows_one + grad_rows_two
    input_grad = (cotangent_own + grad_input_rows).astype(jnp.bfloat16)
    totals = lax.psum(
        (
            grad_gain_one,
            grad_shift_one,
            grad_gain_two,
            grad_shift_two,
            square_context,
            square_active,
        ),
        ("dp", "tensor"),
    )
    token_count = group * lax.axis_size("dp")
    rms_context = jnp.sqrt(totals[4] / (token_count * width))
    rms_active = jnp.sqrt(totals[5] / (token_count * FF))
    return (
        output_rows,
        input_grad,
        grad_qkv,
        grad_out,
        grad_up,
        grad_down,
        totals[0],
        totals[1],
        totals[2],
        totals[3],
        rms_context,
        rms_active,
    )


def solution(mesh):
    return jax.shard_map(
        per_device,
        mesh=mesh,
        in_specs=(
            P(("dp", "tensor"), None),
            P("dp", None),
            P(None, None, "tensor"),
            P("tensor", None),
            P(None, "tensor"),
            P("tensor", None),
            P(),
            P(),
            P(),
            P(),
            P(("dp", "tensor"), None),
        ),
        out_specs=(
            P(("dp", "tensor"), None),
            P(("dp", "tensor"), None),
            P(None, None, "tensor"),
            P("tensor", None),
            P(None, "tensor"),
            P("tensor", None),
            P(),
            P(),
            P(),
            P(),
            P(),
            P(),
        ),
        check_vma=False,
    )
```

profile of v0, /device:TPU:0, one launch (start us, length us, event | category | flops | bytes accessed | tf_op | source)
XLA Modules:
  0.0 632.0 jit_solution(1336476344825085339)
XLA Ops:
  10.5 2.4 fusion.60
  14.5 2.6 copy.25
  18.1 43.4 %all-gather.4.cloned.1.call-done = bf16[1024,1024]{1,0:T(8,128)(2,1)} async-done(((bf16[256,1024]{1,0:T(8,128)(2,1)}), bf16[1024,1024]{1,0:T(8,128)(2,1)}) %all-gather.4.cloned.1.call-update) | async-done | bytes 2097168 | tf_op jit(solution)/shard_map/all_gather | solution.py:97
  61.5 3.9 fusion.77
  66.7 27.1 %while.27 = (s32[]{:T(128)}, f32[2,512,4,64]{1,3,2,0:T(8,128)}, f32[2,4,512]{2,1,0:T(4,128)S(1)}, s32[2]{0:T(128)S(1)}, s32[1024]{0:T(1024)S(1)}, /*index=5*/s32...) while((s32[]{:T(128)}, f32[2,512,4,64]{1,3,2,0:T(8,128)}, ...), condition=%wide.region_7.8_spmd, body=%wide.region_4.7_spmd.sunk | while | flops 563608064 | bytes 29178548 | solution.py:122
  70.5 3.0 fusion.136
  73.5 2.3 fusion.137
  75.9 4.3 fusion.138
  84.1 3.0 fusion.136
  87.0 2.3 fusion.137
  89.4 4.4 fusion.138
  93.7 13.8 %all-gather.8.cloned.1.call-done = bf16[1024,1024]{1,0:T(8,128)(2,1)} async-done(((bf16[256,1024]{1,0:T(8,128)(2,1)}), bf16[1024,1024]{1,0:T(8,128)(2,1)}) %all-gather.8.cloned.1.call-update) | async-done | bytes 2097168 | tf_op jit(solution)/shard_map/all_gather | solution.py:135
  107.5 3.1 convolution_convert_fusion
  110.7 76.4 %while.28 = (s32[]{:T(128)}, f32[1024,4,64]{0,2,1:T(8,128)}, f32[1024,4,64]{0,2,1:T(8,128)}, f32[2,512,4,64]{1,0,3,2:T(2,128)}, s32[2]{0:T(128)S(1)}, /*index=5*...) while((s32[]{:T(128)}, f32[1024,4,64]{0,2,1:T(8,128)}, ...), condition=%wide.region_11.12_spmd.clone, body=%wide.region_9.11_spmd.clone.sunk | while | flops 1376647680 | bytes 162601328 | solution.py:183
  114.7 2.4 fusion.148
  117.2 4.7 multiply_reduce_fusion.4
  121.9 2.4 multiply_convert_fusion.2
  129.1 10.4 %dynamic_update_slice.19 = f32[2,512,4,64]{1,0,3,2:T(2,128)} dynamic-update-slice(f32[2,512,4,64]{1,0,3,2:T(2,128)} %get-tuple-element.450, f32[1,512,4,64]{1,0,3,2:T(1,128)} %copy.51, s32[]{:T(128)} %get-tuple-element.447, s32[]{:T(128)} %constant.73.clone.1..sunk.1, s32[]{:T(128)} %constant.73.clone.1..sunk.1, s32[]{:T(128)} %constant.73.clone.1..sunk.1) | dynamic-update-slice | bytes 1048580 | tf_op jit(solution)/shard_map/while/body/jit(dynamic_update_index_in_dim)/dynamic_update_slice | solution.py:122
  139.5 4.3 fusion.150
  144.7 3.6 fusion.151
  152.1 2.4 fusion.148
  154.5 4.7 multiply_reduce_fusion.4
  159.3 2.4 multiply_convert_fusion.2
  166.4 10.4 %dynamic_update_slice.19 = f32[2,512,4,64]{1,0,3,2:T(2,128)} dynamic-update-slice(f32[2,512,4,64]{1,0,3,2:T(2,128)} %get-tuple-element.450, f32[1,512,4,64]{1,0,3,2:T(1,128)} %copy.51, s32[]{:T(128)} %get-tuple-element.447, s32[]{:T(128)} %constant.73.clone.1..sunk.1, s32[]{:T(128)} %constant.73.clone.1..sunk.1, s32[]{:T(128)} %constant.73.clone.1..sunk.1) | dynamic-update-slice | bytes 1048580 | tf_op jit(solution)/shard_map/while/body/jit(dynamic_update_index_in_dim)/dynamic_update_slice | solution.py:122
  176.8 4.6 fusion.150
  182.2 4.6 fusion.151
  187.1 3.2 stack_reshape.3
  194.5 3.9 fusion.79
  198.5 13.7 %multiply_reduce_fusion.1 = (f32[]{:T(128)}, f32[1024,1024]{1,0:T(8,128)S(1)}, f32[1024,1024]{1,0:T(8,128)S(1)}) fusion(bf16[1024,1024]{1,0:T(8,128)(2,1)} %all-gather.6.cloned.1.call-done, bf16[1024,1024]{1,0:T(8,128)(2,1)S(1)} %copy-done), kind=kOutput, calls=%fused_computation.48 | convolution fusion | flops 2216689664 | bytes 12582916 | tf_op jit(solution)/shard_map/dot_general | solution.py:126
  212.2 4.9 add_convert_fusion
  218.4 4.4 fusion.80
  223.2 2.5 multiply_reduce_fusion.2
  226.3 4.6 fusion.78
  231.0 2.7 convolution_add_fusion
  233.7 3.3 fusion.81
  237.0 5.8 fusion.45
  242.8 4.4 fusion.82
  247.3 4.4 fusion.83
  251.7 22.5 %reduce-scatter.6.cloned.1.call-done = f32[256,1024]{1,0:T(8,128)} async-done(((f32[1024,1024]{1,0:T(8,128)}), f32[256,1024]{1,0:T(8,128)}) %reduce-scatter.6.cloned.1.call-update) | async-done | bytes 1048592 | tf_op jit(solution)/shard_map/reduce_scatter | solution.py:204
  274.2 80.0 %reduce-scatter.8.cloned.1.call-done = f32[256,1024]{1,0:T(8,128)} async-done(((f32[1024,1024]{1,0:T(8,128)}), f32[256,1024]{1,0:T(8,128)}) %reduce-scatter.8.cloned.1.call-update) | async-done | bytes 1048592 | tf_op jit(solution)/shard_map/reduce_scatter | solution.py:205
  354.3 2.0 fusion.75
  356.3 2.4 fusion.64
  358.8 45.2 %all-reduce.3 = (f32[1024]{0:T(1024)}, f32[1024]{0:T(1024)}, f32[1024]{0:T(1024)}, f32[1024]{0:T(1024)}, f32[]{:T(128)}, /*index=5*/f32[]{:T(128)}) all-reduce(f32[1024]{0:T(1024)S(1)} %get-tuple-element.177, f32[1024]{0:T(1024)S(1)} %get-tuple-element.174, ...), channel_id=1, replica_groups=mesh['dp'=8,'tensor'=4] {'dp','tensor'}, use_global_device_ids=true, to_apply=%region_23.24 | all-reduce | flops 4098 | bytes 32784 | tf_op jit(solution)/shard_map/psum | solution.py:211
  405.4 29.4 %reduce-scatter.4.cloned.1.call-done = f32[256,1024]{1,0:T(8,128)} async-done(((f32[1024,1024]{1,0:T(8,128)}), f32[256,1024]{1,0:T(8,128)}) %reduce-scatter.4.cloned.1.call-update) | async-done | bytes 1048592 | tf_op jit(solution)/shard_map/reduce_scatter | solution.py:133
  434.8 3.4 add_convert_fusion.1
  438.2 173.6 %all-reduce.7.cloned.1.call-done = (f32[1024,3,256]{2,0,1:T(8,128)}, f32[256,1024]{1,0:T(8,128)}, f32[1024,1024]{1,0:T(8,128)}, f32[1024,1024]{1,0:T(8,128)}) async-done(((f32[1024,3,256]{2,0,1:T(8,128)}, f32[256,1024]{1,0:T(8,128)}, f32[1024,1024]{1,0:T(8,128)}, f32[1024,1024]{1,0:T(8,128)}), (f32[1024,3,256]{2,0,1:T(8,128)}, f32[256,1024]{1,0:T(8,128)}, f32[1024,1024]{1,0:T(8,128)}, ...) | async-done | bytes 12582928 | tf_op jit(solution)/shard_map/psum | solution.py:200
  611.9 3.9 copy.80
  616.7 2.1 copy.82
  (161 shorter events, 37.3 us)
Async XLA Ops:
  7.2 191.3 %copy-start = (bf16[1024,1024]{1,0:T(8,128)(2,1)S(1)}, bf16[1024,1024]{1,0:T(8,128)(2,1)}, u32[]{:S(2)}) copy-start(bf16[1024,1024]{1,0:T(8,128)(2,1)} %param.19) | copy-start | bytes 6291460
  7.2 9.9 %copy-start.16 = (s32[1,1024]{1,0:T(1,128)S(1)}, s32[1,1024]{1,0:T(1,128)}, u32[]{:S(2)}) copy-start(s32[1,1024]{1,0:T(1,128)} %param.16) | copy-start | bytes 12292
  7.2 54.3 %all-gather.4.cloned.1.call-start = ((), (), s32[]{:S(2)}) async-start(), calls=%async_computation.3 | async-start | bytes 2621440 | tf_op jit(solution)/shard_map/all_gather | solution.py:97
  8.6 1.9 copy-start.27
  10.5 2.4 copy-start.29
  12.9 94.6 %all-gather.8.cloned.1.call-start = ((), (), s32[]{:S(2)}) async-start(), calls=%async_computation.6 | async-start | bytes 2621440 | tf_op jit(solution)/shard_map/all_gather | solution.py:135
  13.7 184.8 %all-gather.6.cloned.1.call-start = ((), (), s32[]{:S(2)}) async-start(), calls=%async_computation.4 | async-start | bytes 2621440 | tf_op jit(solution)/shard_map/all_gather | solution.py:98
  14.4 259.8 %reduce-scatter.6.cloned.1.call-start = ((), (), s32[]{:S(2)}) async-start(), calls=%async_computation.7 | async-start | bytes 5242880 | tf_op jit(solution)/shard_map/reduce_scatter | solution.py:204
  18.1 47.3 %copy-start.19 = (f32[1024,8]{0,1:T(8,128)}, f32[1024,8]{0,1:T(8,128)S(1)}, u32[]{:S(2)}) copy-start(f32[1024,8]{0,1:T(8,128)S(1)} %get-tuple-element.254) | copy-start | bytes 98308
  18.1 47.3 %copy-start.21 = (f32[1024,8]{0,1:T(8,128)}, f32[1024,8]{0,1:T(8,128)S(1)}, u32[]{:S(2)}) copy-start(f32[1024,8]{0,1:T(8,128)S(1)} %get-tuple-element.255) | copy-start | bytes 98308
  66.7 40.8 %copy-start.23 = (bf16[256,1024]{1,0:T(8,128)(2,1)S(1)}, bf16[256,1024]{1,0:T(8,128)(2,1)}, u32[]{:S(2)}) copy-start(bf16[256,1024]{1,0:T(8,128)(2,1)} %param.18) | copy-start | bytes 1572868
  114.7 2.5 copy-start.9
  117.1 4.8 copy-start.1
  124.3 2.0 copy-start.3
  139.5 5.2 copy-start.2
  139.5 5.2 copy-start.10
  152.1 2.4 copy-start.9
  154.5 4.8 copy-start.1
  161.7 2.0 copy-start.3
  176.8 5.4 copy-start.2
  176.8 5.5 copy-start.10
  187.1 4.8 copy-start.4
  187.1 4.8 copy-start.20
  187.1 4.8 copy-start.22
  190.3 1.7 copy-start.6
  192.0 1.2 copy-start.17
  192.0 2.5 copy-start.15
  198.4 155.8 %reduce-scatter.8.cloned.1.call-start = ((), (), s32[]{:S(2)}) async-start(), calls=%async_computation.8 | async-start | bytes 5242880 | tf_op jit(solution)/shard_map/reduce_scatter | solution.py:205
  198.5 13.7 %copy-start.11 = (bf16[1024,1024]{1,0:T(8,128)(2,1)S(1)}, bf16[1024,1024]{1,0:T(8,128)(2,1)}, u32[]{:S(2)}) copy-start(bf16[1024,1024]{1,0:T(8,128)(2,1)} %all-gather.8.cloned.1.call-done) | copy-start | bytes 6291460
  198.5 13.7 %copy-start.33 = (bf16[1024,1024]{1,0:T(8,128)(2,1)S(1)}, bf16[1024,1024]{1,0:T(8,128)(2,1)}, u32[]{:S(2)}) copy-start(bf16[1024,1024]{1,0:T(8,128)(2,1)} %param.20) | copy-start | bytes 6291460
  217.1 1.3 copy-start.36
  222.9 211.9 %reduce-scatter.4.cloned.1.call-start = ((), (), s32[]{:S(2)}) async-start(), calls=%async_computation.5 | async-start | bytes 5242880 | tf_op jit(solution)/shard_map/reduce_scatter | solution.py:133
  226.3 4.6 copy-start.24
  233.7 378.2 %all-reduce.7.cloned.1.call-start = ((), (), s32[]{:S(2)}) async-start(), calls=%async_computation.9 | async-start | bytes 25165824 | tf_op jit(solution)/shard_map/psum | solution.py:200
  237.0 5.8 copy-start.34
  237.0 5.8 copy-start.37
  242.8 4.4 copy-start.12
  242.8 4.4 copy-start.35
  251.6 102.6 %copy-start.5 = (bf16[256,1024]{1,0:T(8,128)(2,1)S(1)}, bf16[256,1024]{1,0:T(8,128)(2,1)}, u32[]{:S(2)}) copy-start(bf16[256,1024]{1,0:T(8,128)(2,1)} %param.15) | copy-start | bytes 1572868
  251.6 102.6 %copy-start.25 = (f32[1024]{0:T(1024)S(1)}, f32[1024]{0:T(1024)}, u32[]{:S(2)}) copy-start(f32[1024]{0:T(1024)} %param.21) | copy-start | bytes 12292
  251.6 102.6 %copy-start.26 = (f32[1024]{0:T(1024)S(1)}, f32[1024]{0:T(1024)}, u32[]{:S(2)}) copy-start(f32[1024]{0:T(1024)} %param.23) | copy-start | bytes 12292
  251.6 102.6 %copy-start.28 = (f32[256]{0:T(256)S(1)}, f32[256]{0:T(256)}, u32[]{:S(2)}) copy-start(f32[256]{0:T(256)} %copy-done.27) | copy-start | bytes 3076
  251.6 104.7 %copy-start.32 = (f32[256]{0:T(256)S(1)}, f32[256]{0:T(256)}, u32[]{:S(2)}) copy-start(f32[256]{0:T(256)} %copy-done.31) | copy-start | bytes 3076
  251.7 104.7 %copy-start.30 = (f32[256]{0:T(256)S(1)}, f32[256]{0:T(256)}, u32[]{:S(2)}) copy-start(f32[256]{0:T(256)} %copy-done.29) | copy-start | bytes 3076
  251.7 183.1 %copy-start.13 = (bf16[256,1024]{1,0:T(8,128)(2,1)S(1)}, bf16[256,1024]{1,0:T(8,128)(2,1)}, u32[]{:S(2)}) copy-start(bf16[256,1024]{1,0:T(8,128)(2,1)} %param.25) | copy-start | bytes 1572868
  611.8 3.9 copy-start.18
  611.8 4.9 copy-start.8
  616.7 3.7 copy-start.7
  (2 other events, 1.7 us)
Sparse Core Ops, SparseCore 0:
  13.0 48.3 all-gather.3
  63.0 44.4 all-gather.7
  109.7 44.5 all-gather.5
  198.6 75.6 reduce-scatter.5
  276.9 77.2 reduce-scatter.7
  356.4 78.3 reduce-scatter.3
  439.4 172.4 all-reduce.6
where the time goes:
time: 641 us; the launch traced here: 632 us
  waiting for transfers between devices  364 us (57%)
  matrix products  108 us (17%)
  local copies, waits for them, and re-layouts  54.4 us (8%)
  blocking collectives  45.2 us (7%)
  other arithmetic  32.8 us (5%)
  between operations  18.6 us (3%)
  loops' own time  8.33 us (1%)
    psum x1, waiting for transfers between devices, per_device(): lax.psum((grad_qkv, grad_out, grad_up, grad_down), 'dp')  174 us
    reduce_scatter x1, waiting for transfers between devices, per_device(): lax.psum_scatter(grad_normed_two, 'tensor', scatter_dimension=0, tiled=True)  80 us
    psum x1, blocking collectives, per_device(): lax.psum((grad_gain_one, grad_shift_one, grad_gain_two, grad_shift_two, s...  45.2 us
    all_gather x1, waiting for transfers between devices, per_device(): lax.all_gather(normed_full_one.astype(jnp.bfloat16), 'tensor', axis=0, ti...  43.4 us
    reduce_scatter x1, waiting for transfers between devices, per_device(): lax.psum_scatter(partial_rows, 'tensor', scatter_dimension=0, tiled=True)  29.4 us
    dynamic_update_slice x4, local copies, waits for them, and re-layouts, per_device(): context_blocks, log_totals = lax.map(forward_block, block_starts)  23.4 us
    reduce_scatter x1, waiting for transfers between devices, per_device(): lax.psum_scatter(grad_normed_one, 'tensor', scatter_dimension=0, tiled=True)  22.5 us
    unnamed x72, local copies, waits for them, and re-layouts  17.4 us
  transfers between devices with their start and end apart: 7, of which 6 were waited for; matrix products, arithmetic and copies ran while one was open for 27% of the time, Pallas kernels for 0%

commit v1 on v0

v1 whole, which is shorter than its diff:
```python
from functools import partial, reduce

import jax
import jax.numpy as jnp
from jax import lax
from jax.experimental import pallas as pl
from jax.experimental.pallas import tpu as pltpu
from jax.sharding import PartitionSpec as P

HS = 64
ROT = 16
FF = 4096
BLOCK = 256
LONGEST = 512
LANES = 128

epsilon = 1e-05
rotary_base = 10000.0
masked_score = -1000000000.0
low = jnp.bfloat16
full = jnp.float32
MESH = pl.DeviceIdType.MESH


def dot(a, b, over_a, over_b):
    return lax.dot_general(
        a, b, (((over_a,), (over_b,)), ((), ())), preferred_element_type=jnp.float32
    )


def total(parts):
    return reduce(jnp.add, parts)


def unit_rows(values):
    average = jnp.mean(values, axis=-1, keepdims=True)
    centred = values - average
    variance = jnp.mean(centred * centred, axis=-1, keepdims=True)
    scale = lax.rsqrt(variance + epsilon)
    return centred * scale, scale


def block_rows(index):
    return slice(index * BLOCK, (index + 1) * BLOCK)


def key_blocks(index):
    reach = (LONGEST + BLOCK - 2) // BLOCK
    return range(max(0, index - reach), index + 1)


def scores_turned(query, keys, seg_col, seg_row, head, at, key_at):
    scores = dot(keys[head, block_rows(key_at), :], query, 1, 1) * HS ** (-0.5)
    allowed = seg_col[block_rows(key_at), :] == seg_row[:, block_rows(at)]
    if at == key_at:
        key_index = lax.broadcasted_iota(jnp.int32, (BLOCK, BLOCK), 0)
        query_index = lax.broadcasted_iota(jnp.int32, (BLOCK, BLOCK), 1)
        allowed = allowed & (key_index <= query_index)
    return jnp.where(allowed, scores, masked_score)


def remote(source, target, send, receive, **device):
    return pltpu.make_async_remote_copy(
        source, target, send, receive, device_id=device, device_id_type=MESH
    )


class DataSum:
    def __init__(self, spots, bufs, send, receive):
        self.part, self.done, self.half, self.a1, self.b1, self.a2, self.b2 = bufs
        self.core, self.x, self.y, self.nx = spots
        self.send, self.receive = send, receive
        rows = self.part.shape[0]
        self.rows = rows
        self.open = []

    def dp(self, core=None, x=None, y=None):
        core = self.core if core is None else core
        x = self.x if x is None else x
        y = self.y if y is None else y
        return (y * self.nx + x) * 2 + core

    def rows_at(self, start, size):
        return pl.ds(pl.multiple_of(start, size), size)

    def put(self, source, target, base, mine, peer, device):
        copy = remote(
            source, target, self.send.at[base + peer], self.receive.at[base + mine], dp=device
        )
        copy.start()
        self.open.append(copy)

    def take(self, target, base, peer):
        remote(
            target, target, self.send.at[base + peer], self.receive.at[base + peer],
            dp=self.dp(),
        ).wait_recv()

    def drain(self):
        for copy in self.open:
            copy.wait_send()
        self.open = []

    def x_peers(self):
        return [lax.rem(self.x + step, self.nx) for step in range(1, self.nx)]

    def bases(self):
        nx = self.nx
        names = {}
        at = 0
        for name, size in (
            ("c", 2), ("a1", nx), ("b1", 2), ("a2", 2), ("b2", nx),
            ("a3", 2), ("b3", nx), ("a4", nx), ("b4", 2), ("d", 2),
        ):
            names[name] = at
            at += size
        names["all"] = at
        return names

    def stage(self, number):
        rows, nx, core, x, y = self.rows, self.nx, self.core, self.x, self.y
        base = self.bases()
        half, quarter, eighth = rows // 2, rows // 4, rows // 8
        a_size, b_size, tail = quarter // nx, eighth, eighth // nx
        other, across = 1 - core, 1 - y
        start = core * half
        if number == 0:
            self.put(
                self.part.at[self.rows_at(other * half, half), :], self.half,
                base["c"], core, other, self.dp(core=other),
            )
        if number == 1:
            self.take(self.half, base["c"], other)
            add_rows(
                self.half, 0, [(self.part, start), (self.half, 0)], half
            )
            self.drain()
            for peer in self.x_peers():
                self.put(
                    self.half.at[self.rows_at(peer * a_size, a_size), :], self.a1.at[x],
                    base["a1"], x, peer, self.dp(x=peer),
                )
            self.put(
                self.half.at[self.rows_at(quarter + across * b_size, b_size), :], self.b1.at[y],
                base["b1"], y, across, self.dp(y=across),
            )
        if number == 2:
            for peer in self.x_peers():
                self.take(self.a1.at[peer], base["a1"], peer)
            add_rows(
                self.half, x * a_size,
                [(self.half, x * a_size)] + [(self.a1.at[peer], 0) for peer in self.x_peers()],
                a_size,
            )
            self.take(self.b1.at[across], base["b1"], across)
            add_rows(
                self.half, quarter + y * b_size,
                [(self.half, quarter + y * b_size), (self.b1.at[across], 0)],
                b_size,
            )
            self.drain()
            self.put(
                self.half.at[self.rows_at(x * a_size + across * tail, tail), :], self.a2.at[y],
                base["a2"], y, across, self.dp(y=across),
            )
            for peer in self.x_peers():
                self.put(
                    self.half.at[self.rows_at(quarter + y * b_size + peer * tail, tail), :],
                    self.b2.at[x], base["b2"], x, peer, self.dp(x=peer),
                )
        if number == 3:
            a_own = x * a_size + y * tail
            b_own = quarter + y * b_size + x * tail
            self.take(self.a2.at[across], base["a2"], across)
            add_rows(
                self.done, start + a_own, [(self.half, a_own), (self.a2.at[across], 0)], tail
            )
            for peer in self.x_peers():
                self.take(self.b2.at[peer], base["b2"], peer)
            add_rows(
                self.done, start + b_own,
                [(self.half, b_own)] + [(self.b2.at[peer], 0) for peer in self.x_peers()],
                tail,
            )
            self.drain()
            piece = self.done.at[self.rows_at(start + a_own, tail), :]
            self.put(piece, piece, base["a3"], y, across, self.dp(y=across))
            piece = self.done.at[self.rows_at(start + b_own, tail), :]
            for peer in self.x_peers():
                self.put(piece, piece, base["b3"], x, peer, self.dp(x=peer))
        if number == 4:
            self.take(
                self.done.at[self.rows_at(start + x * a_size + across * tail, tail), :],
                base["a3"], across,
            )
            for peer in self.x_peers():
                self.take(
                    self.done.at[
                        self.rows_at(start + quarter + y * b_size + peer * tail, tail), :
                    ],
                    base["b3"], peer,
                )
            self.drain()
            piece = self.done.at[self.rows_at(start + x * a_size, a_size), :]
            for peer in self.x_peers():
                self.put(piece, piece, base["a4"], x, peer, self.dp(x=peer))
            piece = self.done.at[self.rows_at(start + quarter + y * b_size, b_size), :]
            self.put(piece, piece, base["b4"], y, across, self.dp(y=across))
        if number == 5:
            for peer in self.x_peers():
                self.take(
                    self.done.at[self.rows_at(start + peer * a_size, a_size), :],
                    base["a4"], peer,
                )
            self.take(
                self.done.at[self.rows_at(start + quarter + across * b_size, b_size), :],
                base["b4"], across,
            )
            self.drain()
            piece = self.done.at[self.rows_at(start, half), :]
            self.put(piece, piece, base["d"], core, other, self.dp(core=other))
        if number == 6:
            self.take(self.done.at[self.rows_at(other * half, half), :], base["d"], other)
            self.drain()


def add_rows(target, target_start, sources, size):
    step = min(size, 64)

    def one(index, carry):
        offset = index * step

        def rows(start):
            return pl.ds(pl.multiple_of(start + offset, min(step, 16)), step)

        summed = total([ref[rows(start), :].astype(full) for ref, start in sources])
        target[rows(target_start), :] = summed.astype(target.dtype)
        return carry

    lax.fori_loop(0, size // step, one, 0)


def layer_kernel(
    ring,
    ranks,
    tokens, cotangent, seg_col, seg_row, norms, w_qkv, w_out, w_up, w_down,
    output_rows, input_grad, grad_down_out, grad_up_out, grad_mix_out, vectors_out,
    wq, wo, wu, wd, weight_sem, out_sem,
    x_all, g_all, normed_one, normed_two, active, slope, u_all,
    acc_down, acc_up, queries, keys, values, grad_context, context, logs,
    grad_q, turn_cos, turn_sin,
    gather_send, gather_recv,
    branch_buf, branch_send, branch_recv, grad_buf, grad_send, grad_recv,
    part0, done0, half0, a10, b10, a20, b20,
    done1, half1, a11, b11, a21, b21,
    data_send, data_recv,
    vectors, vec_tensor, vec_core, vec_x, vec_y, vec_send, vec_recv,
):
    group = x_all.shape[0]
    width = x_all.shape[1]
    shard = group // ring
    heads = queries.shape[0]
    local = heads * HS
    blocks = group // BLOCK
    hidden_local = wu.shape[1]
    nx = ranks // 4
    part1 = wu
    grad_proj = normed_two
    t = lax.axis_index("tensor")
    dp = lax.axis_index("dp")
    core = lax.rem(dp, 2)
    x_at = lax.rem(dp // 2, nx)
    y_at = dp // (2 * nx)
    spots = (core, x_at, y_at, nx)

    def rows(s):
        return pl.ds(pl.multiple_of(s * shard, shard), shard)

    def dp_of(c, x, y):
        return (y * nx + x) * 2 + c

    weights = [
        pltpu.make_async_copy(source, target, weight_sem.at[index])
        for index, (source, target) in enumerate(
            ((w_qkv, wq), (w_up, wu), (w_out, wo), (w_down, wd))
        )
    ]
    for copy in weights:
        copy.start()

    barrier = pltpu.get_barrier_semaphore()
    peers = [dict(tensor=lax.rem(t + step, ring)) for step in range(1, ring)]
    peers.append(dict(dp=dp_of(1 - core, x_at, y_at)))
    peers.append(dict(dp=dp_of(core, x_at, 1 - y_at)))
    for step in range(1, nx):
        peers.append(dict(dp=dp_of(core, lax.rem(x_at + step, nx), y_at)))
    for peer in peers:
        pl.semaphore_signal(barrier, inc=1, device_id=peer, device_id_type=MESH)
    pl.semaphore_wait(barrier, len(peers))

    def relay(which, source, s, side):
        target = (x_all, g_all)[which].at[rows(s), :]
        return remote(
            source,
            target,
            gather_send.at[which, side, s],
            gather_recv.at[which, s],
            tensor=t + 1 if side == 0 else t - 1,
        )

    def arrive(which, s):
        target = (x_all, g_all)[which].at[rows(s), :]
        remote(
            target, target, gather_send.at[which, 0, s], gather_recv.at[which, s], tensor=t
        ).wait_recv()

    def gather_step(which, k):
        array = (x_all, g_all)[which]

        @pl.when((k > 0) & (t - k >= 0))
        def _():
            s = t - k
            arrive(which, s)

            @pl.when(t < ring - 1)
            def _():
                relay(which, array.at[rows(s), :], s, 0).start()

        @pl.when((k > 0) & (t + k < ring))
        def _():
            s = t + k
            arrive(which, s)

            @pl.when(t > 0)
            def _():
                relay(which, array.at[rows(s), :], s, 1).start()

    def gather_own(which, side):
        relay(which, (tokens, cotangent)[which], t, side).start()

    def gather_drain(which):
        array = (x_all, g_all)[which]

        def one(s, carry):
            @pl.when((s <= t) & (t < ring - 1))
            def _():
                relay(which, array.at[rows(s), :], s, 0).wait_send()

            @pl.when((s >= t) & (t > 0))
            def _():
                relay(which, array.at[rows(s), :], s, 1).wait_send()

            return carry

        lax.fori_loop(0, ring, one, 0)

    @pl.when(t < ring - 1)
    def _():
        gather_own(0, 0)

    @pl.when(t > 0)
    def _():
        gather_own(0, 1)

    x_all[rows(t), :] = tokens[...]
    g_all[rows(t), :] = cotangent[...]
    vectors[...] = jnp.zeros_like(vectors)
    acc_down[...] = jnp.zeros_like(acc_down)
    acc_up[...] = jnp.zeros_like(acc_up)
    gain_one, shift_one = norms[0:1, :], norms[1:2, :]
    gain_two, shift_two = norms[2:3, :], norms[3:4, :]
    for copy in weights:
        copy.wait()

    lane = lax.broadcasted_iota(jnp.int32, (shard, LANES), 1) % HS

    def turned(part, cosine, sine):
        moved = jnp.where(
            lane < ROT // 2, pltpu.roll(part, LANES - ROT // 2, 1), pltpu.roll(part, ROT // 2, 1)
        )
        return part * cosine + moved * sine

    def forward_rows(s):
        at = rows(s)
        unit, _ = unit_rows(x_all[at, :].astype(full))
        one = (unit * gain_one + shift_one).astype(low)
        two = (unit * gain_two + shift_two).astype(low)
        normed_one[at, :] = one
        normed_two[at, :] = two
        own_segments = seg_col[at, :]
        before = jnp.sum((seg_row[...] < own_segments).astype(jnp.int32), axis=1, keepdims=True)
        index = lax.broadcasted_iota(jnp.int32, (shard, 1), 0) + s * shard
        position = (index - before).astype(full)
        angle = position * norms[4:5, 0:LANES]
        cosine = jnp.cos(angle)
        sine = jnp.sin(angle) * norms[5:6, 0:LANES]
        turn_cos[at, :] = cosine
        turn_sin[at, :] = sine
        projected = dot(one, wq[...], 1, 0)
        for index_part, ref in enumerate((queries, keys, values)):
            for pair in range(local // LANES):
                lo = index_part * local + pair * LANES
                part = projected[:, lo : lo + LANES]
                if index_part < 2:
                    part = turned(part, cosine, sine)
                part = part.astype(low)
                for side in range(LANES // HS):
                    ref[pair * (LANES // HS) + side, at, :] = part[:, side * HS : (side + 1) * HS]
        hidden = dot(two, wu[...], 1, 0)
        inner = 0.5 * (1.0 + lax.erf(hidden * 0.7071067811865476))
        activated = hidden * inner
        steep = inner + hidden * jnp.exp(-0.5 * hidden * hidden) * 0.3989422804014327
        active[at, :] = activated.astype(low)
        for chunk in range(hidden_local // LANES):
            slope[chunk, at, :] = steep[:, chunk * LANES : (chunk + 1) * LANES]
        vectors[4:5, 0:hidden_local] += jnp.sum(activated * activated, axis=0, keepdims=True)

    def both_sides(k, body):
        def one(side, carry):
            s = jnp.where(side == 0, t - k, t + k)

            @pl.when((s >= 0) & (s < ring) & ((k > 0) | (side == 0)))
            def _():
                body(s)

            return carry

        lax.fori_loop(0, 2, one, 0)

    def forward_step(k, carry):
        gather_step(0, k)

        @pl.when((k == t) & (t < ring - 1))
        def _():
            gather_own(1, 0)

        @pl.when((k == ring - 1 - t) & (t > 0))
        def _():
            gather_own(1, 1)

        both_sides(k, forward_rows)
        return carry

    lax.fori_loop(0, ring, forward_step, 0)

    for at in range(blocks):

        def forward_head(head, carry, at=at):
            query = queries[head, block_rows(at), :]
            spans = key_blocks(at)
            scores = [
                scores_turned(query, keys, seg_col, seg_row, head, at, span) for span in spans
            ]
            most = reduce(jnp.maximum, [jnp.max(s, axis=0, keepdims=True) for s in scores])
            raised = [jnp.exp(s - most) for s in scores]
            summed = total([jnp.sum(e, axis=0, keepdims=True) for e in raised])
            share = 1.0 / summed
            logs[head, :, block_rows(at)] = most + jnp.log(summed)
            mixed = total(
                [
                    dot((e * share).astype(low), values[head, block_rows(span), :], 0, 0)
                    for e, span in zip(raised, spans)
                ]
            )
            context[head, block_rows(at), :] = mixed.astype(low)
            vectors[5:6, 0:HS] += jnp.sum(mixed * mixed, axis=0, keepdims=True)
            return carry

        lax.fori_loop(0, heads, forward_head, 0)

    def heads_side_by_side(ref, at):
        return jnp.concatenate([ref[head, at, :] for head in range(heads)], axis=1)

    def branch_rows(s):
        at = rows(s)
        return dot(heads_side_by_side(context, at), wo[...], 1, 0) + dot(
            active[at, :], wd[...], 1, 0
        )

    def chain(buffer, send, receive, make):
        def hop(s, side):
            if side == 0:
                slot = s
            else:
                slot = jnp.where(s == t - 1, ring, s)
            return remote(
                buffer.at[s],
                buffer.at[slot],
                send.at[s],
                receive.at[slot],
                tensor=t + 1 if side == 0 else t - 1,
            )

        def landed(slot):
            remote(buffer.at[slot], buffer.at[slot], send.at[0], receive.at[slot], tensor=t).wait_recv()

        def pass_on(s, side):
            has = t > 0 if side == 0 else t < ring - 1

            @pl.when(has)
            def _():
                landed(s)
                buffer[s] = (make(s) + buffer[s].astype(full)).astype(low)

            @pl.when(jnp.logical_not(has))
            def _():
                buffer[s] = make(s).astype(low)

            hop(s, side).start()

        def own():
            value = make(t)
            carried = [value]

            @pl.when(t > 0)
            def _():
                landed(t)

            @pl.when(t < ring - 1)
            def _():
                landed(ring)

            left = jnp.where(t > 0, buffer[t].astype(full), 0.0)
            right = jnp.where(t < ring - 1, buffer[ring].astype(full), 0.0)
            return value + left + right

        def drain():
            def one(s, carry):
                @pl.when(s > t)
                def _():
                    hop(s, 0).wait_send()

                @pl.when(s < t)
                def _():
                    hop(s, 1).wait_send()

                return carry

            lax.fori_loop(0, ring, one, 0)

        return pass_on, own, drain

    branch_pass, branch_own, branch_drain = chain(
        branch_buf, branch_send, branch_recv, branch_rows
    )

    def backward_rows(s):
        at = rows(s)
        grad = g_all[at, :]
        grad_active = dot(grad, wd[...], 1, 1)
        steep = jnp.concatenate(
            [slope[chunk, at, :] for chunk in range(hidden_local // LANES)], axis=1
        )
        grad_hidden = (grad_active * steep).astype(low)
        for block in range(hidden_local // BLOCK):
            acc_down[block_rows(block), :] += dot(active[at, block_rows(block)], grad, 0, 0)
        for block in range(width // BLOCK):
            acc_up[block_rows(block), :] += dot(
                normed_two[at, block_rows(block)], grad_hidden, 0, 0
            )
        grad_two = dot(grad_hidden, wu[...], 1, 1)
        unit, _ = unit_rows(x_all[at, :].astype(full))
        vectors[2:3, 0:width] += jnp.sum(grad_two * unit, axis=0, keepdims=True)
        vectors[3:4, 0:width] += jnp.sum(grad_two, axis=0, keepdims=True)
        u_all[at, :] = grad_two * gain_two
        back = dot(grad, wo[...], 1, 1).astype(low)
        for head in range(heads):
            grad_context[head, at, :] = back[:, head * HS : (head + 1) * HS]

    def backward_step(k, carry):
        gather_step(1, k)

        s_up = ring - 1 - k + t

        @pl.when((s_up > t) & (s_up < ring))
        def _():
            branch_pass(s_up, 0)

        s_down = k - (ring - 1 - t)

        @pl.when((s_down >= 0) & (s_down < t))
        def _():
            branch_pass(s_down, 1)

        both_sides(k, backward_rows)
        return carry

    lax.fori_loop(0, ring, backward_step, 0)

    def narrow(source, target):
        step = 64

        def one(index, carry):
            at = pl.ds(pl.multiple_of(index * step, step), step)
            target[at, :] = source[at, :].astype(low)
            return carry

        lax.fori_loop(0, source.shape[0] // step, one, 0)

    down_sum = DataSum(
        spots, (part0, done0, half0, a10, b10, a20, b20), data_send.at[0], data_recv.at[0]
    )
    up_sum = DataSum(
        spots, (part1, done1, half1, a11, b11, a21, b21), data_send.at[1], data_recv.at[1]
    )
    narrow(acc_down, part0)
    down_sum.stage(0)
    narrow(acc_up, part1)
    up_sum.stage(0)

    output_rows[...] = (tokens[...].astype(full) + branch_own()).astype(low)

    def u_rows(s):
        return u_all[rows(s), :]

    grad_pass, grad_own, grad_drain = chain(grad_buf, grad_send, grad_recv, u_rows)

    def grad_chain_step(j):
        s_up = ring - 1 - j + t

        @pl.when((s_up > t) & (s_up < ring))
        def _():
            grad_pass(s_up, 0)

        s_down = 2 * (ring - 1) - t - j

        @pl.when((s_down >= 0) & (s_down < t))
        def _():
            grad_pass(s_down, 1)

    grad_keys = slope
    slots = [
        lambda: (down_sum.stage(1), up_sum.stage(1)),
        lambda: (down_sum.stage(2),),
        lambda: (up_sum.stage(2), down_sum.stage(3)),
        lambda: (up_sum.stage(3), down_sum.stage(4)),
    ]
    step_done = 0
    for at in reversed(range(blocks)):

        def backward_head(head, carry, at=at):
            query = queries[head, block_rows(at), :]
            grad = grad_context[head, block_rows(at), :]
            spans = key_blocks(at)
            log_total = logs[head, :, block_rows(at)]
            probs = [
                jnp.exp(
                    scores_turned(query, keys, seg_col, seg_row, head, at, span) - log_total
                )
                for span in spans
            ]
            grad_probs = [dot(values[head, block_rows(span), :], grad, 1, 1) for span in spans]
            inner = total(
                [jnp.sum(p * d, axis=0, keepdims=True) for p, d in zip(probs, grad_probs)]
            )
            grad_query = []
            for p, d, span in zip(probs, grad_probs, spans):
                grad_scores = (p * (d - inner)).astype(low)
                grad_value = dot(p.astype(low), grad, 1, 0)
                grad_key = dot(grad_scores, query, 1, 0) * HS ** (-0.5)
                grad_query.append(dot(grad_scores, keys[head, block_rows(span), :], 0, 0))
                if at == min(span + len(key_blocks(blocks)) - 1, blocks - 1):
                    grad_keys[2 * head, block_rows(span), 0:HS] = grad_key
                    grad_keys[2 * head + 1, block_rows(span), 0:HS] = grad_value
                else:
                    grad_keys[2 * head, block_rows(span), 0:HS] += grad_key
                    grad_keys[2 * head + 1, block_rows(span), 0:HS] += grad_value
            grad_q[head] = total(grad_query) * HS ** (-0.5)
            return carry

        lax.fori_loop(0, heads, backward_head, 0)

        per_block = BLOCK // shard
        for piece in reversed(range(per_block)):
            s = at * per_block + piece
            at_rows = slice(s * shard, (s + 1) * shard)
            inside = slice(piece * shard, (piece + 1) * shard)
            cosine = turn_cos[at_rows, :]
            sine = -turn_sin[at_rows, :]
            grads = []
            for index_part in range(3):
                for pair in range(local // LANES):
                    if index_part == 0:
                        halves = [grad_q[2 * pair + e, inside, :] for e in range(2)]
                    else:
                        halves = [
                            grad_keys[2 * (2 * pair + e) + index_part - 1, at_rows, 0:HS]
                            for e in range(2)
                        ]
                    part = jnp.concatenate(halves, axis=1)
                    if index_part < 2:
                        part = turned(part, cosine, sine)
                    grads.append(part.astype(low))
            projected = jnp.concatenate(grads, axis=1)
            grad_proj[at_rows, 0 : 3 * local] = projected
            grad_one = dot(projected, wq[...], 1, 1)
            unit, _ = unit_rows(x_all[at_rows, :].astype(full))
            vectors[0:1, 0:width] += jnp.sum(grad_one * unit, axis=0, keepdims=True)
            vectors[1:2, 0:width] += jnp.sum(grad_one, axis=0, keepdims=True)
            u_all[at_rows, :] += grad_one * gain_one
            grad_chain_step(step_done)
            step_done += 1
        if slots:
            for _ in slots.pop(0)():
                pass

    while slots:
        slots.pop(0)()

    def vec_put(slots_ref, base, mine, peer, device):
        return remote(
            vectors,
            slots_ref.at[mine],
            vec_send.at[base + peer],
            vec_recv.at[base + mine],
            **device,
        )

    def vec_round(slots_ref, base, mine, size, device_of):
        others = [lax.rem(mine + step, size) for step in range(1, size)]
        for peer in others:
            vec_put(slots_ref, base, mine, peer, device_of(peer)).start()
        slots_ref[mine] = vectors[...]

        def finish():
            for peer in others:
                vec_put(slots_ref, base, mine, peer, device_of(peer)).wait_send()
                remote(
                    slots_ref.at[peer], slots_ref.at[peer],
                    vec_send.at[base + peer], vec_recv.at[base + peer], tensor=t,
                ).wait_recv()
            vectors[...] = total([slots_ref[index] for index in range(size)])

        return finish

    finish_vec = vec_round(vec_tensor, 0, t, ring, lambda peer: dict(tensor=peer))

    up_sum.stage(4)
    down_sum.stage(5)
    up_sum.stage(5)
    down_sum.stage(6)
    copy_down = pltpu.make_async_copy(done0, grad_down_out, out_sem.at[0])
    copy_down.start()
    part_mix, done_mix = part1, done1
    for block in range(width // BLOCK):
        part_mix[block_rows(block), 0 : 3 * local] = dot(
            normed_one[:, block_rows(block)], grad_proj[:, 0 : 3 * local], 0, 0
        ).astype(low)
    up_sum.stage(6)
    copy_up = pltpu.make_async_copy(done1, grad_up_out, out_sem.at[1])
    copy_up.start()
    copy_up.wait()
    copy_down.wait()
    for block in range(width // local):
        cols = slice(block * local, (block + 1) * local)
        part_mix[cols, 3 * local :] = dot(
            heads_side_by_side(context, slice(None)), g_all[:, cols], 0, 0
        ).astype(low)
    mix_sum = DataSum(
        spots, (part_mix, done_mix, half1, a11, b11, a21, b21), data_send.at[2], data_recv.at[2]
    )
    mix_sum.stage(0)
    finish_vec()
    finish_vec = vec_round(
        vec_core, ring, core, 2, lambda peer: dict(dp=dp_of(peer, x_at, y_at))
    )
    grad_chain_step(ring)
    mix_sum.stage(1)
    finish_vec()
    finish_vec = vec_round(
        vec_x, ring + 2, x_at, nx, lambda peer: dict(dp=dp_of(core, peer, y_at))
    )
    mix_sum.stage(2)
    finish_vec()
    finish_vec = vec_round(
        vec_y, ring + 2 + nx, y_at, 2, lambda peer: dict(dp=dp_of(core, x_at, peer))
    )
    for j in range(ring + 1, 2 * ring - 2):
        grad_chain_step(j)
    mix_sum.stage(3)
    finish_vec()
    rows_all = group * ranks
    rms_active = jnp.sqrt(jnp.sum(vectors[4:5, :], axis=1, keepdims=True) / (rows_all * FF))
    rms_context = jnp.sqrt(jnp.sum(vectors[5:6, :], axis=1, keepdims=True) / (rows_all * width))
    vectors_out[0:4, :] = vectors[0:4, :]
    vectors_out[4:5, :] = jnp.broadcast_to(rms_context, (1, vectors.shape[1]))
    vectors_out[5:6, :] = jnp.broadcast_to(rms_active, (1, vectors.shape[1]))
    vectors_out[6:8, :] = jnp.zeros_like(vectors_out[6:8, :])
    mix_sum.stage(4)
    weighted = grad_own()
    unit, scale = unit_rows(tokens[...].astype(full))
    grad_rows = scale * (
        weighted
        - jnp.mean(weighted, axis=-1, keepdims=True)
        - unit * jnp.mean(weighted * unit, axis=-1, keepdims=True)
    )
    input_grad[...] = (cotangent[...].astype(full) + grad_rows).astype(low)
    mix_sum.stage(5)
    mix_sum.stage(6)
    copy_mix = pltpu.make_async_copy(done_mix, grad_mix_out, out_sem.at[2])
    copy_mix.start()
    gather_drain(0)
    gather_drain(1)
    branch_drain()
    grad_drain()
    copy_mix.wait()


def per_device(
    ring, ranks,
    tokens, segments, w_qkv, w_out, w_up, w_down,
    gain_one, shift_one, gain_two, shift_two, cotangent,
):
    shard, width = tokens.shape
    group = segments.shape[1]
    local = w_qkv.shape[2]
    heads = local // HS
    hidden_local = w_up.shape[1]
    nx = ranks // 4
    half_rot = ROT // 2
    lane = jnp.arange(width) % HS
    frequency = rotary_base ** (-(2.0 * (lane % half_rot).astype(jnp.float32)) / ROT)
    frequency = jnp.where(lane < ROT, frequency, 0.0)
    sign = jnp.where(lane < half_rot, -1.0, 1.0)
    zero = jnp.zeros((width,), jnp.float32)
    norms = jnp.stack([gain_one, shift_one, gain_two, shift_two, frequency, sign, zero, zero])
    vmem = pl.BlockSpec(memory_space=pltpu.VMEM)
    anywhere = pl.BlockSpec(memory_space=pl.ANY)
    wide = max(width, hidden_local)
    scratch = lambda *shape: pltpu.VMEM(shape, low)
    wider = lambda *shape: pltpu.VMEM(shape, full)
    sems = lambda *shape: pltpu.SemaphoreType.DMA(shape)

    def sum_buffers(rows, columns):
        return [
            scratch(rows, columns),
            scratch(rows, columns),
            scratch(rows // 2, columns),
            scratch(nx, rows // (4 * nx), columns),
            scratch(2, rows // 8, columns),
            scratch(2, rows // (8 * nx), columns),
            scratch(nx, rows // (8 * nx), columns),
        ]

    data_sems = 12 + 4 * nx
    outs = pl.pallas_call(
        partial(layer_kernel, ring, ranks),
        name="layer",
        out_shape=[
            jax.ShapeDtypeStruct((shard, width), low),
            jax.ShapeDtypeStruct((shard, width), low),
            jax.ShapeDtypeStruct((hidden_local, width), low),
            jax.ShapeDtypeStruct((width, hidden_local), low),
            jax.ShapeDtypeStruct((width, 4 * local), low),
            jax.ShapeDtypeStruct((8, wide), full),
        ],
        in_specs=[vmem] * 5 + [anywhere] * 4,
        out_specs=[vmem, vmem, anywhere, anywhere, anywhere, vmem],
        scratch_shapes=[
            scratch(width, 3 * local), scratch(local, width),
            scratch(width, hidden_local), scratch(hidden_local, width),
            sems(4), sems(3),
            scratch(group, width), scratch(group, width),
            scratch(group, width), scratch(group, width),
            scratch(group, hidden_local),
            wider(hidden_local // LANES, group, LANES),
            wider(group, width),
            wider(hidden_local, width), wider(width, hidden_local),
            scratch(heads, group, HS), scratch(heads, group, HS), scratch(heads, group, HS),
            scratch(heads, group, HS), scratch(heads, group, HS),
            wider(heads, 1, group),
            wider(heads, BLOCK, HS),
            wider(group, LANES), wider(group, LANES),
            sems(2, 2, ring), sems(2, ring),
            scratch(ring + 1, shard, width), sems(ring), sems(ring + 1),
            scratch(ring + 1, shard, width), sems(ring), sems(ring + 1),
            *sum_buffers(hidden_local, width),
            *sum_buffers(width, hidden_local)[1:],
            sems(3, data_sems), sems(3, data_sems),
            wider(8, wide), wider(ring, 8, wide), wider(2, 8, wide),
            wider(nx, 8, wide), wider(2, 8, wide),
            sems(ring + 4 + nx), sems(ring + 4 + nx),
        ],
        compiler_params=pltpu.CompilerParams(
            collective_id=0, has_side_effects=True, vmem_limit_bytes=67043328
        ),
    )(
        tokens, cotangent, segments.reshape(group, 1), segments, norms,
        w_qkv.reshape(width, 3 * local), w_out, w_up, w_down,
    )
    output_rows, input_grad, grad_down, grad_up, grad_mix, vectors = outs
    grad_qkv = grad_mix[:, : 3 * local].astype(jnp.float32).reshape(width, 3, local)
    grad_out = (
        grad_mix[:, 3 * local :]
        .reshape(width // local, local, local)
        .transpose(1, 0, 2)
        .reshape(local, width)
        .astype(jnp.float32)
    )
    return (
        output_rows,
        input_grad,
        grad_qkv,
        grad_out,
        grad_up.astype(jnp.float32),
        grad_down.astype(jnp.float32),
        vectors[0, :width],
        vectors[1, :width],
        vectors[2, :width],
        vectors[3, :width],
        vectors[4, 0],
        vectors[5, 0],
    )


def solution(mesh):
    everyone = P(("dp", "tensor"), None)
    return jax.shard_map(
        partial(per_device, mesh.shape["tensor"], mesh.shape["dp"]),
        mesh=mesh,
        in_specs=(
            everyone,
            P("dp", None),
            P(None, None, "tensor"),
            P("tensor", None),
            P(None, "tensor"),
            P("tensor", None),
            P(),
            P(),
            P(),
            P(),
            everyone,
        ),
        out_specs=(
            everyone,
            everyone,
            P(None, None, "tensor"),
            P("tensor", None),
            P(None, "tensor"),
            P("tensor", None),
            P(),
            P(),
            P(),
            P(),
            P(),
            P(),
        ),
        check_vma=False,
    )
```

time: 641 us -> 207 us (0.32); the launches traced: 632 us -> 206 us
  waiting for transfers between devices: 364 us -> 0 us
  Pallas kernels: 0 us -> 180 us
  matrix products: 108 us -> 0 us
  blocking collectives: 45.2 us -> 0 us
  local copies, waits for them, and re-layouts: 54.4 us -> 19.8 us
  other arithmetic: 32.8 us -> 5.32 us
  between operations: 18.6 us -> 0.71 us
  loops' own time: 8.33 us -> 0 us
    pallas_call x0 -> x1, Pallas kernels: none -> 180 us  [per_device(): pl.pallas_call(partial(layer_kernel, ring, ranks), name='layer', out_shap...]
    psum x1 -> x0, waiting for transfers between devices: 174 us -> none  [per_device(): lax.psum((grad_qkv, grad_out, grad_up, grad_down), 'dp')]
    reduce_scatter x3 -> x0, waiting for transfers between devices: 132 us -> none  [the longest x1 80 us: per_device(): lax.psum_scatter(grad_normed_two, 'tensor', scatter_dimension=0, tiled=True)]
    dot_general x26 -> x0, matrix products: 108 us -> none  [the longest x1 13.7 us: per_device(): hidden = jnp.dot(normed_two, w_up, preferred_element_type=jnp.float32)]
    all_gather x3 -> x0, waiting for transfers between devices: 57.2 us -> none  [the longest x1 43.4 us: per_device(): lax.all_gather(normed_full_one.astype(jnp.bfloat16), 'tensor', axis=0, ti...]
    psum x1 -> x0, blocking collectives: 45.2 us -> none  [per_device(): lax.psum((grad_gain_one, grad_shift_one, grad_gain_two, grad_shift_two, s...]
    dynamic_update_slice x4 -> x0, local copies, waits for them, and re-layouts: 23.4 us -> none  [per_device(): context_blocks, log_totals = lax.map(forward_block, block_starts)]
    reduce_sum x7 -> x0, other arithmetic: 14.3 us -> none  [the longest x2 4.67 us: forward_block(): total_exp = jnp.sum(weights_exp, axis=-1, keepdims=True)]
  transfers between devices with their start and end apart: 7 -> 0, of which waited for: 6 -> 0; matrix products, arithmetic and copies ran while one was open for 27% -> 0% of each run, Pallas kernels for 0% -> 0%
where the time goes in v1:
time: 207 us; the launch traced here: 206 us
  Pallas kernels  180 us (87%)
  local copies, waits for them, and re-layouts  19.8 us (10%)
  other arithmetic  5.32 us (3%)
    pallas_call x1, Pallas kernels, per_device(): pl.pallas_call(partial(layer_kernel, ring, ranks), name='layer', out_shap...  180 us
    unnamed x14, local copies, waits for them, and re-layouts  7.76 us

profile of v1, /device:TPU:0, one launch (start us, length us, event | category | flops | bytes accessed | tf_op | source)
XLA Modules:
  0.0 206.3 jit_solution(9171096544413236457)
XLA Ops:
  0.7 1.4 stack.25.norms
  2.1 1.7 copy.27.seg_col
  3.8 1.7 copy.26
  5.5 1.6 copy.28.w_qkv
  7.1 180.5 %layer.1 = (bf16[256,1024]{1,0:T(8,128)(2,1)}, bf16[256,1024]{1,0:T(8,128)(2,1)}, bf16[1024,1024]{1,0:T(8,128)(2,1)}, bf16[1024,1024]{1,0:T(8,128)(2,1)}, bf16[1024,1024]{1,0:T(8,128)(2,1)}, /*index=5*/f32[8,1024]{1,0:T(8,128)}) custom-call(bf16[256,1024]{1,0:T(8,128)(2,1)} %tokens.1, bf16[256,1024]{1,0:T(8,128)(2,1)} %cotangent.1, s32[1024,1]{1,0:T(8,128)} %copy.27.seg_col, ...), custom_call_target="tpu_custom_call" | custom-call | tf_op jit(solution)/shard_map/layer/pallas_call | solution.py:846
  187.5 1.3 fusion.6
  188.8 1.5 fusion.7
  190.3 1.1 slice.25
  191.4 0.0 copy-start.2
  191.4 0.1 convert_bitcast_fusion
  191.5 1.1 copy.32
  192.6 0.8 copy-done.2
  193.4 0.2 slice_convert_fusion
  193.6 2.4 %copy.29 = f32[1024,768]{0,1:T(8,128)} copy(f32[1024,768]{1,0:T(8,128)S(1)} %slice_convert_fusion) | data formatting | bytes 6291456 | tf_op jit(solution)/shard_map/reshape | solution.py:892
  196.0 0.0 copy-start.1
  196.0 3.7 %copy.31 = f32[1024,3,256]{2,0,1:T(8,128)} copy(f32[1024,3,256]{0,2,1:T(8,128)} %bitcast.19) | data formatting | bytes 6291456
  199.7 0.0 copy-done.1
  199.7 0.0 copy-start
  199.7 2.5 %convert_element_type.34 = f32[1024,1024]{1,0:T(8,128)} convert(bf16[1024,1024]{1,0:T(8,128)(2,1)S(1)} %copy-done.1) | non-fusion elementwise | flops 1048576 | bytes 6291456 | tf_op jit(solution)/shard_map/convert_element_type | solution.py:905
  202.2 0.0 copy-done
  202.2 0.0 copy-start.4
  202.2 0.0 copy-start.3
  202.2 2.5 %convert_element_type.35 = f32[1024,1024]{1,0:T(8,128)} convert(bf16[1024,1024]{1,0:T(8,128)(2,1)S(1)} %copy-done) | non-fusion elementwise | flops 1048576 | bytes 6291456 | tf_op jit(solution)/shard_map/convert_element_type | solution.py:906
  204.7 0.0 copy-done.4
  204.7 0.8 copy.35
  205.5 0.0 copy-done.3
  205.5 0.8 copy.36
  (2 shorter events, 0.0 us)
Async XLA Ops:
  191.4 2.0 copy-start.2
  196.0 3.7 %copy-start.1 = (bf16[1024,1024]{1,0:T(8,128)(2,1)S(1)}, bf16[1024,1024]{1,0:T(8,128)(2,1)}, u32[]{:S(2)}) copy-start(bf16[1024,1024]{1,0:T(8,128)(2,1)} %get-tuple-element.21) | copy-start | bytes 6291460
  199.7 2.5 %copy-start = (bf16[1024,1024]{1,0:T(8,128)(2,1)S(1)}, bf16[1024,1024]{1,0:T(8,128)(2,1)}, u32[]{:S(2)}) copy-start(bf16[1024,1024]{1,0:T(8,128)(2,1)} %get-tuple-element.22) | copy-start | bytes 6291460
  202.2 2.5 %copy-start.4 = (bf16[256,1024]{1,0:T(8,128)(2,1)S(1)}, bf16[256,1024]{1,0:T(8,128)(2,1)}, u32[]{:S(2)}) copy-start(bf16[256,1024]{1,0:T(8,128)(2,1)} %get-tuple-element.68) | copy-start | bytes 1572868
  202.2 3.3 %copy-start.3 = (bf16[256,1024]{1,0:T(8,128)(2,1)S(1)}, bf16[256,1024]{1,0:T(8,128)(2,1)}, u32[]{:S(2)}) copy-start(bf16[256,1024]{1,0:T(8,128)(2,1)} %get-tuple-element.69) | copy-start | bytes 1572868

commit v2 on v1

--- a/solution.py
+++ b/solution.py
@@ -2,6 +2,7 @@
 
 import jax
 import jax.numpy as jnp
+import numpy as np
 from jax import lax
 from jax.experimental import pallas as pl
 from jax.experimental.pallas import tpu as pltpu
@@ -49,9 +50,9 @@
     return range(max(0, index - reach), index + 1)
 
 
-def scores_turned(query, keys, seg_col, seg_row, head, at, key_at):
+def scores_turned(query, keys, seg_col, segment_row, head, at, key_at):
     scores = dot(keys[head, block_rows(key_at), :], query, 1, 1) * HS ** (-0.5)
-    allowed = seg_col[block_rows(key_at), :] == seg_row[:, block_rows(at)]
+    allowed = seg_col[block_rows(key_at), :] == segment_row[:, block_rows(at)]
     if at == key_at:
         key_index = lax.broadcasted_iota(jnp.int32, (BLOCK, BLOCK), 0)
         query_index = lax.broadcasted_iota(jnp.int32, (BLOCK, BLOCK), 1)
@@ -100,6 +101,9 @@
         for copy in self.open:
             copy.wait_send()
         self.open = []
+
+    def seat(self, sender, receiver):
+        return lax.rem(sender - receiver - 1 + 2 * self.nx, self.nx)
 
     def x_peers(self):
         return [lax.rem(self.x + step, self.nx) for step in range(1, self.nx)]
@@ -137,49 +141,49 @@
             self.drain()
             for peer in self.x_peers():
                 self.put(
-                    self.half.at[self.rows_at(peer * a_size, a_size), :], self.a1.at[x],
+                    self.half.at[self.rows_at(peer * a_size, a_size), :], self.a1.at[self.seat(x, peer)],
                     base["a1"], x, peer, self.dp(x=peer),
                 )
             self.put(
-                self.half.at[self.rows_at(quarter + across * b_size, b_size), :], self.b1.at[y],
+                self.half.at[self.rows_at(quarter + across * b_size, b_size), :], self.b1.at[0],
                 base["b1"], y, across, self.dp(y=across),
             )
         if number == 2:
             for peer in self.x_peers():
-                self.take(self.a1.at[peer], base["a1"], peer)
+                self.take(self.a1.at[self.seat(peer, x)], base["a1"], peer)
             add_rows(
                 self.half, x * a_size,
-                [(self.half, x * a_size)] + [(self.a1.at[peer], 0) for peer in self.x_peers()],
+                [(self.half, x * a_size)] + [(self.a1.at[self.seat(peer, x)], 0) for peer in self.x_peers()],
                 a_size,
             )
-            self.take(self.b1.at[across], base["b1"], across)
+            self.take(self.b1.at[0], base["b1"], across)
             add_rows(
                 self.half, quarter + y * b_size,
-                [(self.half, quarter + y * b_size), (self.b1.at[across], 0)],
+                [(self.half, quarter + y * b_size), (self.b1.at[0], 0)],
                 b_size,
             )
             self.drain()
             self.put(
-                self.half.at[self.rows_at(x * a_size + across * tail, tail), :], self.a2.at[y],
+                self.half.at[self.rows_at(x * a_size + across * tail, tail), :], self.a2.at[0],
                 base["a2"], y, across, self.dp(y=across),
             )
             for peer in self.x_peers():
                 self.put(
                     self.half.at[self.rows_at(quarter + y * b_size + peer * tail, tail), :],
-                    self.b2.at[x], base["b2"], x, peer, self.dp(x=peer),
+                    self.b2.at[self.seat(x, peer)], base["b2"], x, peer, self.dp(x=peer),
                 )
         if number == 3:
             a_own = x * a_size + y * tail
             b_own = quarter + y * b_size + x * tail
-            self.take(self.a2.at[across], base["a2"], across)
+            self.take(self.a2.at[0], base["a2"], across)
             add_rows(
-                self.done, start + a_own, [(self.half, a_own), (self.a2.at[across], 0)], tail
+                self.done, start + a_own, [(self.half, a_own), (self.a2.at[0], 0)], tail
             )
             for peer in self.x_peers():
-                self.take(self.b2.at[peer], base["b2"], peer)
+                self.take(self.b2.at[self.seat(peer, x)], base["b2"], peer)
             add_rows(
                 self.done, start + b_own,
-                [(self.half, b_own)] + [(self.b2.at[peer], 0) for peer in self.x_peers()],
+                [(self.half, b_own)] + [(self.b2.at[self.seat(peer, x)], 0) for peer in self.x_peers()],
                 tail,
             )
             self.drain()
@@ -243,16 +247,18 @@
 def layer_kernel(
     ring,
     ranks,
-    tokens, cotangent, seg_col, seg_row, norms, w_qkv, w_out, w_up, w_down,
-    output_rows, input_grad, grad_down_out, grad_up_out, grad_mix_out, vectors_out,
-    wq, wo, wu, wd, weight_sem, out_sem,
-    x_all, g_all, normed_one, normed_two, active, slope, u_all,
+    tokens, cotangent, seg_row, gains_one, shifts_one, gains_two, shifts_two, table,
+    w_qkv, w_out, w_up, w_down,
+    output_rows, input_grad, grad_down_out, grad_up_out, grad_qkv_out, grad_out_out, vectors_out,
+    wq, wo, wu, wd, load_sem, out_sem,
+    seg_col, x_all, g_all, normed_two, active, slope, u_all,
     acc_down, acc_up, queries, keys, values, grad_context, context, logs,
     grad_q, turn_cos, turn_sin,
     gather_send, gather_recv,
     branch_buf, branch_send, branch_recv, grad_buf, grad_send, grad_recv,
     part0, done0, half0, a10, b10, a20, b20,
     done1, half1, a11, b11, a21, b21,
+    done2, half2, a12, b12, a22, b22,
     data_send, data_recv,
     vectors, vec_tensor, vec_core, vec_x, vec_y, vec_send, vec_recv,
 ):
@@ -263,6 +269,7 @@
     local = heads * HS
     blocks = group // BLOCK
     hidden_local = wu.shape[1]
+    hidden_part = min(hidden_local, BLOCK)
     nx = ranks // 4
     part1 = wu
     grad_proj = normed_two
@@ -279,13 +286,16 @@
     def dp_of(c, x, y):
         return (y * nx + x) * 2 + c
 
-    weights = [
-        pltpu.make_async_copy(source, target, weight_sem.at[index])
-        for index, (source, target) in enumerate(
-            ((w_qkv, wq), (w_up, wu), (w_out, wo), (w_down, wd))
-        )
+    pairs = [(tokens, x_all.at[rows(t), :]), (cotangent, g_all.at[rows(t), :])]
+    pairs += [
+        (w_qkv.at[part], wq.at[:, part * local : (part + 1) * local]) for part in range(3)
     ]
-    for copy in weights:
+    pairs += [(w_up, wu), (w_out, wo), (w_down, wd)]
+    loads = [
+        pltpu.make_async_copy(source, target, load_sem.at[index])
+        for index, (source, target) in enumerate(pairs)
+    ]
+    for copy in loads:
         copy.start()
 
     barrier = pltpu.get_barrier_semaphore()
@@ -362,14 +372,14 @@
     def _():
         gather_own(0, 1)
 
-    x_all[rows(t), :] = tokens[...]
-    g_all[rows(t), :] = cotangent[...]
+    segment_row = seg_row[...].astype(full)
+    seg_col[...] = jnp.broadcast_to(segment_row, (LANES, group)).T[:, 0:1]
     vectors[...] = jnp.zeros_like(vectors)
     acc_down[...] = jnp.zeros_like(acc_down)
     acc_up[...] = jnp.zeros_like(acc_up)
-    gain_one, shift_one = norms[0:1, :], norms[1:2, :]
-    gain_two, shift_two = norms[2:3, :], norms[3:4, :]
-    for copy in weights:
+    gain_one, shift_one = gains_one[...], shifts_one[...]
+    gain_two, shift_two = gains_two[...], shifts_two[...]
+    for copy in loads:
         copy.wait()
 
     lane = lax.broadcasted_iota(jnp.int32, (shard, LANES), 1) % HS
@@ -385,15 +395,14 @@
         unit, _ = unit_rows(x_all[at, :].astype(full))
         one = (unit * gain_one + shift_one).astype(low)
         two = (unit * gain_two + shift_two).astype(low)
-        normed_one[at, :] = one
         normed_two[at, :] = two
         own_segments = seg_col[at, :]
-        before = jnp.sum((seg_row[...] < own_segments).astype(jnp.int32), axis=1, keepdims=True)
+        before = jnp.sum((segment_row < own_segments).astype(jnp.int32), axis=1, keepdims=True)
         index = lax.broadcasted_iota(jnp.int32, (shard, 1), 0) + s * shard
         position = (index - before).astype(full)
-        angle = position * norms[4:5, 0:LANES]
+        angle = position * table[0:1, :]
         cosine = jnp.cos(angle)
-        sine = jnp.sin(angle) * norms[5:6, 0:LANES]
+        sine = jnp.sin(angle) * table[1:2, :]
         turn_cos[at, :] = cosine
         turn_sin[at, :] = sine
         projected = dot(one, wq[...], 1, 0)
@@ -406,14 +415,16 @@
                 part = part.astype(low)
                 for side in range(LANES // HS):
                     ref[pair * (LANES // HS) + side, at, :] = part[:, side * HS : (side + 1) * HS]
-        hidden = dot(two, wu[...], 1, 0)
-        inner = 0.5 * (1.0 + lax.erf(hidden * 0.7071067811865476))
-        activated = hidden * inner
-        steep = inner + hidden * jnp.exp(-0.5 * hidden * hidden) * 0.3989422804014327
-        active[at, :] = activated.astype(low)
-        for chunk in range(hidden_local // LANES):
-            slope[chunk, at, :] = steep[:, chunk * LANES : (chunk + 1) * LANES]
-        vectors[4:5, 0:hidden_local] += jnp.sum(activated * activated, axis=0, keepdims=True)
+        for lo in range(0, hidden_local, hidden_part):
+            span = slice(lo, lo + hidden_part)
+            hidden = dot(two, wu[:, span], 1, 0)
+            inner = 0.5 * (1.0 + lax.erf(hidden * 0.7071067811865476))
+            activated = hidden * inner
+            steep = inner + hidden * jnp.exp(-0.5 * hidden * hidden) * 0.3989422804014327
+            active[at, span] = activated.astype(low)
+            for chunk in range(hidden_part // LANES):
+                slope[lo // LANES + chunk, at, :] = steep[:, chunk * LANES : (chunk + 1) * LANES]
+            vectors[4:5, span] += jnp.sum(activated * activated, axis=0, keepdims=True)
 
     def both_sides(k, body):
         def one(side, carry):
@@ -449,7 +460,7 @@
             query = queries[head, block_rows(at), :]
             spans = key_blocks(at)
             scores = [
-                scores_turned(query, keys, seg_col, seg_row, head, at, span) for span in spans
+                scores_turned(query, keys, seg_col, segment_row, head, at, span) for span in spans
             ]
             most = reduce(jnp.maximum, [jnp.max(s, axis=0, keepdims=True) for s in scores])
             raised = [jnp.exp(s - most) for s in scores]
@@ -510,7 +521,6 @@
 
         def own():
             value = make(t)
-            carried = [value]
 
             @pl.when(t > 0)
             def _():
@@ -547,18 +557,18 @@
     def backward_rows(s):
         at = rows(s)
         grad = g_all[at, :]
-        grad_active = dot(grad, wd[...], 1, 1)
-        steep = jnp.concatenate(
-            [slope[chunk, at, :] for chunk in range(hidden_local // LANES)], axis=1
-        )
-        grad_hidden = (grad_active * steep).astype(low)
-        for block in range(hidden_local // BLOCK):
-            acc_down[block_rows(block), :] += dot(active[at, block_rows(block)], grad, 0, 0)
-        for block in range(width // BLOCK):
-            acc_up[block_rows(block), :] += dot(
-                normed_two[at, block_rows(block)], grad_hidden, 0, 0
-            )
-        grad_two = dot(grad_hidden, wu[...], 1, 1)
+        grad_two = None
+        for lo in range(0, hidden_local, hidden_part):
+            span = slice(lo, lo + hidden_part)
+            steep = jnp.concatenate(
+                [slope[lo // LANES + chunk, at, :] for chunk in range(hidden_part // LANES)],
+                axis=1,
+            )
+            grad_hidden = (dot(grad, wd[span, :], 1, 1) * steep).astype(low)
+            acc_down[span, :] += dot(active[at, span], grad, 0, 0)
+            acc_up[:, span] += dot(normed_two[at, :], grad_hidden, 0, 0)
+            more = dot(grad_hidden, wu[:, span], 1, 1)
+            grad_two = more if grad_two is None else grad_two + more
         unit, _ = unit_rows(x_all[at, :].astype(full))
         vectors[2:3, 0:width] += jnp.sum(grad_two * unit, axis=0, keepdims=True)
         vectors[3:4, 0:width] += jnp.sum(grad_two, axis=0, keepdims=True)
@@ -570,17 +580,13 @@
     def backward_step(k, carry):
         gather_step(1, k)
 
-        s_up = ring - 1 - k + t
-
-        @pl.when((s_up > t) & (s_up < ring))
+        @pl.when((t == 0) & (k < ring - 1))
         def _():
-            branch_pass(s_up, 0)
-
-        s_down = k - (ring - 1 - t)
-
-        @pl.when((s_down >= 0) & (s_down < t))
+            branch_pass(ring - 1 - k, 0)
+
+        @pl.when((t == ring - 1) & (k < ring - 1))
         def _():
-            branch_pass(s_down, 1)
+            branch_pass(k, 1)
 
         both_sides(k, backward_rows)
         return carry
@@ -603,12 +609,27 @@
     up_sum = DataSum(
         spots, (part1, done1, half1, a11, b11, a21, b21), data_send.at[1], data_recv.at[1]
     )
+    def branch_hop(p):
+        s_up = ring - 2 - p + t
+
+        @pl.when((t > 0) & (s_up > t) & (s_up < ring))
+        def _():
+            branch_pass(s_up, 0)
+
+        s_down = p + 2 - ring + t
+
+        @pl.when((t < ring - 1) & (s_down >= 0) & (s_down < t))
+        def _():
+            branch_pass(s_down, 1)
+
     narrow(acc_down, part0)
     down_sum.stage(0)
     narrow(acc_up, part1)
     up_sum.stage(0)
-
-    output_rows[...] = (tokens[...].astype(full) + branch_own()).astype(low)
+    branch_hop(0)
+    branch_hops = list(range(1, ring - 2))
+    down_sum.stage(1)
+    up_sum.stage(1)
 
     def u_rows(s):
         return u_all[rows(s), :]
@@ -616,13 +637,13 @@
     grad_pass, grad_own, grad_drain = chain(grad_buf, grad_send, grad_recv, u_rows)
 
     def grad_chain_step(j):
-        s_up = ring - 1 - j + t
+        s_up = ring - 1 - j + 2 * t
 
         @pl.when((s_up > t) & (s_up < ring))
         def _():
             grad_pass(s_up, 0)
 
-        s_down = 2 * (ring - 1) - t - j
+        s_down = 3 * (ring - 1) - 2 * t - j
 
         @pl.when((s_down >= 0) & (s_down < t))
         def _():
@@ -630,7 +651,6 @@
 
     grad_keys = slope
     slots = [
-        lambda: (down_sum.stage(1), up_sum.stage(1)),
         lambda: (down_sum.stage(2),),
         lambda: (up_sum.stage(2), down_sum.stage(3)),
         lambda: (up_sum.stage(3), down_sum.stage(4)),
@@ -645,7 +665,7 @@
             log_total = logs[head, :, block_rows(at)]
             probs = [
                 jnp.exp(
-                    scores_turned(query, keys, seg_col, seg_row, head, at, span) - log_total
+                    scores_turned(query, keys, seg_col, segment_row, head, at, span) - log_total
                 )
                 for span in spans
             ]
@@ -701,11 +721,14 @@
             grad_chain_step(step_done)
             step_done += 1
         if slots:
-            for _ in slots.pop(0)():
-                pass
+            slots.pop(0)()
+        if branch_hops:
+            branch_hop(branch_hops.pop(0))
 
     while slots:
         slots.pop(0)()
+    for p in branch_hops:
+        branch_hop(p)
 
     def vec_put(slots_ref, base, mine, peer, device):
         return remote(
@@ -735,49 +758,76 @@
 
     finish_vec = vec_round(vec_tensor, 0, t, ring, lambda peer: dict(tensor=peer))
 
-    up_sum.stage(4)
-    down_sum.stage(5)
-    up_sum.stage(5)
-    down_sum.stage(6)
-    copy_down = pltpu.make_async_copy(done0, grad_down_out, out_sem.at[0])
-    copy_down.start()
-    part_mix, done_mix = part1, done1
-    for block in range(width // BLOCK):
-        part_mix[block_rows(block), 0 : 3 * local] = dot(
-            normed_one[:, block_rows(block)], grad_proj[:, 0 : 3 * local], 0, 0
-        ).astype(low)
-    up_sum.stage(6)
-    copy_up = pltpu.make_async_copy(done1, grad_up_out, out_sem.at[1])
-    copy_up.start()
-    copy_up.wait()
-    copy_down.wait()
-    for block in range(width // local):
-        cols = slice(block * local, (block + 1) * local)
+    part_mix = part1
+    gather_drain(1)
+    def out_block(block, carry):
+        cols = pl.ds(pl.multiple_of(block * local, local), local)
         part_mix[cols, 3 * local :] = dot(
             heads_side_by_side(context, slice(None)), g_all[:, cols], 0, 0
         ).astype(low)
+        return carry
+
+    lax.fori_loop(0, width // local, out_block, 0)
+
+    def norm_again(s, carry):
+        unit, _ = unit_rows(x_all[rows(s), :].astype(full))
+        g_all[rows(s), :] = (unit * gain_one + shift_one).astype(low)
+        return carry
+
+    lax.fori_loop(0, ring, norm_again, 0)
+    def mix_block(block, carry):
+        span = pl.ds(pl.multiple_of(block * BLOCK, BLOCK), BLOCK)
+        part_mix[span, 0 : 3 * local] = dot(
+            g_all[:, span], grad_proj[:, 0 : 3 * local], 0, 0
+        ).astype(low)
+        return carry
+
+    lax.fori_loop(0, width // BLOCK, mix_block, 0)
     mix_sum = DataSum(
-        spots, (part_mix, done_mix, half1, a11, b11, a21, b21), data_send.at[2], data_recv.at[2]
+        spots, (part_mix, done2, half2, a12, b12, a22, b22), data_send.at[2], data_recv.at[2]
     )
     mix_sum.stage(0)
+    late = iter(range(ring, 3 * ring - 4))
+
+    def late_step(count=1):
+        for _, j in zip(range(count), late):
+            grad_chain_step(j)
+
+    up_sum.stage(4)
+    late_step()
+    mix_sum.stage(1)
+    down_sum.stage(5)
     finish_vec()
     finish_vec = vec_round(
         vec_core, ring, core, 2, lambda peer: dict(dp=dp_of(peer, x_at, y_at))
     )
-    grad_chain_step(ring)
-    mix_sum.stage(1)
+    late_step()
+    up_sum.stage(5)
+    mix_sum.stage(2)
     finish_vec()
     finish_vec = vec_round(
         vec_x, ring + 2, x_at, nx, lambda peer: dict(dp=dp_of(core, peer, y_at))
     )
-    mix_sum.stage(2)
+    down_sum.stage(6)
+    copies = [pltpu.make_async_copy(done0, grad_down_out, out_sem.at[0])]
+    copies[-1].start()
+    late_step()
+    mix_sum.stage(3)
+    up_sum.stage(6)
+    copies.append(pltpu.make_async_copy(done1, grad_up_out, out_sem.at[1]))
+    copies[-1].start()
     finish_vec()
     finish_vec = vec_round(
         vec_y, ring + 2 + nx, y_at, 2, lambda peer: dict(dp=dp_of(core, x_at, peer))
     )
-    for j in range(ring + 1, 2 * ring - 2):
-        grad_chain_step(j)
-    mix_sum.stage(3)
+    late_step(2 * ring)
+    mix_sum.stage(4)
+    branch_buf[t] = (x_all[rows(t), :].astype(full) + branch_own()).astype(low)
+    copies.append(pltpu.make_async_copy(branch_buf.at[t], output_rows, out_sem.at[2]))
+    copies[-1].start()
+    own_cotangent = branch_buf.at[ring]
+    own_load = pltpu.make_async_copy(cotangent, own_cotangent, load_sem.at[0])
+    own_load.start()
     finish_vec()
     rows_all = group * ranks
     rms_active = jnp.sqrt(jnp.sum(vectors[4:5, :], axis=1, keepdims=True) / (rows_all * FF))
@@ -786,24 +836,73 @@
     vectors_out[4:5, :] = jnp.broadcast_to(rms_context, (1, vectors.shape[1]))
     vectors_out[5:6, :] = jnp.broadcast_to(rms_active, (1, vectors.shape[1]))
     vectors_out[6:8, :] = jnp.zeros_like(vectors_out[6:8, :])
-    mix_sum.stage(4)
     weighted = grad_own()
-    unit, scale = unit_rows(tokens[...].astype(full))
+    own_load.wait()
+    unit, scale = unit_rows(x_all[rows(t), :].astype(full))
     grad_rows = scale * (
         weighted
         - jnp.mean(weighted, axis=-1, keepdims=True)
         - unit * jnp.mean(weighted * unit, axis=-1, keepdims=True)
     )
-    input_grad[...] = (cotangent[...].astype(full) + grad_rows).astype(low)
+    grad_buf[t] = (own_cotangent[...].astype(full) + grad_rows).astype(low)
+    copies.append(pltpu.make_async_copy(grad_buf.at[t], input_grad, out_sem.at[3]))
+    copies[-1].start()
     mix_sum.stage(5)
     mix_sum.stage(6)
-    copy_mix = pltpu.make_async_copy(done_mix, grad_mix_out, out_sem.at[2])
-    copy_mix.start()
+    for part in range(3):
+        copies.append(
+            pltpu.make_async_copy(
+                done2.at[:, part * local : (part + 1) * local],
+                grad_qkv_out.at[part],
+                out_sem.at[4 + part],
+            )
+        )
+        copies[-1].start()
+    for block in range(width // local):
+        cols = slice(block * local, (block + 1) * local)
+        copies.append(
+            pltpu.make_async_copy(
+                done2.at[cols, 3 * local :], grad_out_out.at[:, cols], out_sem.at[7 + block]
+            )
+        )
+        copies[-1].start()
     gather_drain(0)
-    gather_drain(1)
     branch_drain()
     grad_drain()
-    copy_mix.wait()
+    for copy in copies:
+        copy.wait()
+
+
+def widen_kernel(*refs):
+    count = 6
+    for source, target in zip(refs[:count], refs[count + 1 : 2 * count + 1]):
+        target[...] = source[...].astype(target.dtype)
+    vectors = refs[count]
+    for index, target in enumerate(refs[2 * count + 1 :]):
+        target[...] = vectors[index : index + 1, 0 : target.shape[1]]
+
+
+def widen(arrays, vectors, width):
+    steps = 8
+
+    def spec(shape):
+        block = list(shape)
+        block[-2] //= steps
+        lead = (0,) * (len(shape) - 2)
+        return pl.BlockSpec(tuple(block), lambda i, lead=lead: (*lead, i, 0))
+
+    kinds = [low, low, full, full, full, full]
+    small = [(1, width)] * 4 + [(1, 1)] * 2
+    whole = lambda shape: pl.BlockSpec(shape, lambda i: (0, 0))
+    return pl.pallas_call(
+        widen_kernel,
+        name="widen",
+        grid=(steps,),
+        out_shape=[jax.ShapeDtypeStruct(a.shape, kind) for a, kind in zip(arrays, kinds)]
+        + [jax.ShapeDtypeStruct(shape, full) for shape in small],
+        in_specs=[spec(a.shape) for a in arrays] + [whole(vectors.shape)],
+        out_specs=[spec(a.shape) for a in arrays] + [whole(shape) for shape in small],
+    )(*arrays, vectors)
 
 
 def per_device(
@@ -818,12 +917,11 @@
     hidden_local = w_up.shape[1]
     nx = ranks // 4
     half_rot = ROT // 2
-    lane = jnp.arange(width) % HS
-    frequency = rotary_base ** (-(2.0 * (lane % half_rot).astype(jnp.float32)) / ROT)
-    frequency = jnp.where(lane < ROT, frequency, 0.0)
-    sign = jnp.where(lane < half_rot, -1.0, 1.0)
-    zero = jnp.zeros((width,), jnp.float32)
-    norms = jnp.stack([gain_one, shift_one, gain_two, shift_two, frequency, sign, zero, zero])
+    lane = np.arange(LANES) % HS
+    frequency = rotary_base ** (-(2.0 * (lane % half_rot)) / ROT)
+    frequency = np.where(lane < ROT, frequency, 0.0)
+    sign = np.where(lane < half_rot, -1.0, 1.0)
+    table = jnp.asarray(np.stack([frequency, sign] + [np.zeros(LANES)] * 6), jnp.float32)
     vmem = pl.BlockSpec(memory_space=pltpu.VMEM)
     anywhere = pl.BlockSpec(memory_space=pl.ANY)
     wide = max(width, hidden_local)
@@ -836,10 +934,10 @@
             scratch(rows, columns),
             scratch(rows, columns),
             scratch(rows // 2, columns),
-            scratch(nx, rows // (4 * nx), columns),
-            scratch(2, rows // 8, columns),
-            scratch(2, rows // (8 * nx), columns),
-            scratch(nx, rows // (8 * nx), columns),
+            scratch(nx - 1, rows // (4 * nx), columns),
+            scratch(1, rows // 8, columns),
+            scratch(1, rows // (8 * nx), columns),
+            scratch(nx - 1, rows // (8 * nx), columns),
         ]
 
     data_sems = 12 + 4 * nx
@@ -851,17 +949,18 @@
             jax.ShapeDtypeStruct((shard, width), low),
             jax.ShapeDtypeStruct((hidden_local, width), low),
             jax.ShapeDtypeStruct((width, hidden_local), low),
-            jax.ShapeDtypeStruct((width, 4 * local), low),
+            jax.ShapeDtypeStruct((3, width, local), low),
+            jax.ShapeDtypeStruct((local, width), low),
             jax.ShapeDtypeStruct((8, wide), full),
         ],
-        in_specs=[vmem] * 5 + [anywhere] * 4,
-        out_specs=[vmem, vmem, anywhere, anywhere, anywhere, vmem],
+        in_specs=[anywhere] * 2 + [vmem] * 6 + [anywhere] * 4,
+        out_specs=[anywhere] * 6 + [vmem],
         scratch_shapes=[
             scratch(width, 3 * local), scratch(local, width),
             scratch(width, hidden_local), scratch(hidden_local, width),
-            sems(4), sems(3),
-            scratch(group, width), scratch(group, width),
-            scratch(group, width), scratch(group, width),
+            sems(8), sems(7 + width // local),
+            wider(group, 1),
+            scratch(group, width), scratch(group, width), scratch(group, width),
             scratch(group, hidden_local),
             wider(hidden_local // LANES, group, LANES),
             wider(group, width),
@@ -876,6 +975,7 @@
             scratch(ring + 1, shard, width), sems(ring), sems(ring + 1),
             *sum_buffers(hidden_local, width),
             *sum_buffers(width, hidden_local)[1:],
+            *sum_buffers(width, 4 * local)[1:],
             sems(3, data_sems), sems(3, data_sems),
             wider(8, wide), wider(ring, 8, wide), wider(2, 8, wide),
             wider(nx, 8, wide), wider(2, 8, wide),
@@ -885,31 +985,23 @@
             collective_id=0, has_side_effects=True, vmem_limit_bytes=67043328
         ),
     )(
-        tokens, cotangent, segments.reshape(group, 1), segments, norms,
-        w_qkv.reshape(width, 3 * local), w_out, w_up, w_down,
-    )
-    output_rows, input_grad, grad_down, grad_up, grad_mix, vectors = outs
-    grad_qkv = grad_mix[:, : 3 * local].astype(jnp.float32).reshape(width, 3, local)
-    grad_out = (
-        grad_mix[:, 3 * local :]
-        .reshape(width // local, local, local)
-        .transpose(1, 0, 2)
-        .reshape(local, width)
-        .astype(jnp.float32)
+        tokens, cotangent, segments,
+        *(v.reshape(1, width) for v in (gain_one, shift_one, gain_two, shift_two)), table,
+        w_qkv.transpose(1, 0, 2), w_out, w_up, w_down,
+    )
+    output_rows, input_grad, grad_down, grad_up, grad_qkv, grad_out, *small = widen(
+        outs[:6], outs[6], width
     )
     return (
         output_rows,
         input_grad,
-        grad_qkv,
+        grad_qkv.transpose(1, 0, 2),
         grad_out,
-        grad_up.astype(jnp.float32),
-        grad_down.astype(jnp.float32),
-        vectors[0, :width],
-        vectors[1, :width],
-        vectors[2, :width],
-        vectors[3, :width],
-        vectors[4, 0],
-        vectors[5, 0],
+        grad_up,
+        grad_down,
+        *(v.reshape(width) for v in small[:4]),
+        small[4].reshape(()),
+        small[5].reshape(()),
     )
 
 

time: 207 us -> 176 us (0.85)
  local copies, waits for them, and re-layouts: 19.8 us -> 0 us
  other arithmetic: 5.32 us -> 0 us
  Pallas kernels: 180 us -> 175 us
    pallas_call x1, Pallas kernels: 180 us -> 166 us  [per_device(): pl.pallas_call(partial(layer_kernel, ring, ranks), name='layer', out_shap...]
    pallas_call x0 -> x1, Pallas kernels: none -> 9.18 us  [widen(): pl.pallas_call(widen_kernel, name='widen', grid=(steps,), out_shape=[jax....]
    unnamed x14 -> x0, local copies, waits for them, and re-layouts: 7.76 us -> none
    reshape x3 -> x0, local copies, waits for them, and re-layouts: 5.64 us -> none  [the longest x1 2.36 us: per_device(): grad_mix[:, :3 * local].astype(jnp.float32).reshape(width, 3, local)]
    convert_element_type x2 -> x0, other arithmetic: 4.96 us -> none  [the longest x1 2.48 us: per_device(): grad_down.astype(jnp.float32)]
    slice x3 -> x0, local copies, waits for them, and re-layouts: 3.88 us -> none  [the longest x1 1.55 us: per_device(): vectors[3, :width]]
where the time goes in v2:
time: 176 us
  Pallas kernels  175 us (99%)
    pallas_call x1, Pallas kernels, per_device(): pl.pallas_call(partial(layer_kernel, ring, ranks), name='layer', out_shap...  166 us
    pallas_call x1, Pallas kernels, widen(): pl.pallas_call(widen_kernel, name='widen', grid=(steps,), out_shape=[jax....  9.18 us

profile of v2, /device:TPU:0, one launch (start us, length us, event | category | flops | bytes accessed | tf_op | source)
XLA Modules:
  0.0 176.0 jit_solution(17464691755663606935)
XLA Ops:
  0.6 166.0 %layer.1 = (bf16[256,1024]{1,0:T(8,128)(2,1)}, bf16[256,1024]{1,0:T(8,128)(2,1)}, bf16[1024,1024]{1,0:T(8,128)(2,1)}, bf16[1024,1024]{1,0:T(8,128)(2,1)}, bf16[3...) custom-call(bf16[256,1024]{1,0:T(8,128)(2,1)} %tokens.1, bf16[256,1024]{1,0:T(8,128)(2,1)} %cotangent.1, ...), custom_call_target="tpu_custom_call" | custom-call | tf_op jit(solution)/shard_map/layer/pallas_call | solution.py:944
  166.7 9.2 %widen.1 = (bf16[256,1024]{1,0:T(8,128)(2,1)}, bf16[256,1024]{1,0:T(8,128)(2,1)}, f32[1024,1024]{1,0:T(8,128)}, f32[1024,1024]{1,0:T(8,128)}, f32[3,1024,256]{2,...) custom-call(bf16[256,1024]{1,0:T(8,128)(2,1)} %get-tuple-element.31., ...), custom_call_target="tpu_custom_call" | custom-call | tf_op jit(solution)/shard_map/widen/pallas_call | solution.py:897

commit v3 on v2

--- a/solution.py
+++ b/solution.py
@@ -14,6 +14,7 @@
 BLOCK = 256
 LONGEST = 512
 LANES = 128
+PIECES = 1
 
 epsilon = 1e-05
 rotary_base = 10000.0
@@ -631,23 +632,94 @@
     down_sum.stage(1)
     up_sum.stage(1)
 
-    def u_rows(s):
-        return u_all[rows(s), :]
-
-    grad_pass, grad_own, grad_drain = chain(grad_buf, grad_send, grad_recv, u_rows)
-
-    def grad_chain_step(j):
-        s_up = ring - 1 - j + 2 * t
-
-        @pl.when((s_up > t) & (s_up < ring))
+    part_rows = shard // PIECES
+
+    def u_hop(s, piece, side):
+        at = pl.ds(pl.multiple_of(piece * part_rows, part_rows), part_rows)
+        slot = s if side == 0 else jnp.where(s == t - 1, ring, s)
+        return remote(
+            grad_buf.at[s, at, :],
+            grad_buf.at[slot, at, :],
+            grad_send.at[s, piece],
+            grad_recv.at[slot, piece],
+            tensor=t + 1 if side == 0 else t - 1,
+        )
+
+    def u_landed(slot, piece):
+        at = pl.ds(pl.multiple_of(piece * part_rows, part_rows), part_rows)
+        ref = grad_buf.at[slot, at, :]
+        remote(ref, ref, grad_send.at[0, piece], grad_recv.at[slot, piece], tensor=t).wait_recv()
+
+    def each_piece(body):
+        def one(piece, carry):
+            body(piece)
+            return carry
+
+        lax.fori_loop(0, PIECES, one, 0)
+
+    def u_start(s):
+        for side, end in ((0, 0), (1, ring - 1)):
+            if s == end:
+                continue
+
+            @pl.when(t == end)
+            def _(side=side):
+                grad_buf[s] = u_all[rows(s), :].astype(low)
+                each_piece(lambda piece: u_hop(s, piece, side).start())
+
+    def u_pass(s, piece, side):
+        u_landed(s, piece)
+        at = pl.ds(pl.multiple_of(piece * part_rows, part_rows), part_rows)
+        source = pl.ds(pl.multiple_of(s * shard + piece * part_rows, part_rows), part_rows)
+        grad_buf[s, at, :] = (u_all[source, :] + grad_buf[s, at, :].astype(full)).astype(low)
+        u_hop(s, piece, side).start()
+
+    def u_step(tick, carry):
+        up = tick - 2 * t
+        s_up = ring - 1 - up // PIECES
+
+        @pl.when((t > 0) & (up >= 0) & (s_up > t))
         def _():
-            grad_pass(s_up, 0)
-
-        s_down = 3 * (ring - 1) - 2 * t - j
-
-        @pl.when((s_down >= 0) & (s_down < t))
+            u_pass(s_up, lax.rem(up, PIECES), 0)
+
+        down = tick + 2 - 2 * (ring - 1 - t)
+        s_down = ring - 1 - down // PIECES
+
+        @pl.when((t < ring - 1) & (down >= 0) & (s_down >= 0) & (s_down < t))
         def _():
-            grad_pass(s_down, 1)
+            u_pass(s_down, lax.rem(down, PIECES), 1)
+
+        return carry
+
+    def u_steps(first, last):
+        lax.fori_loop(first, last, u_step, 0)
+
+    def u_own():
+        @pl.when(t > 0)
+        def _():
+            each_piece(lambda piece: u_landed(t, piece))
+
+        @pl.when(t < ring - 1)
+        def _():
+            each_piece(lambda piece: u_landed(ring, piece))
+
+        left = jnp.where(t > 0, grad_buf[t].astype(full), 0.0)
+        right = jnp.where(t < ring - 1, grad_buf[ring].astype(full), 0.0)
+        return u_all[rows(t), :] + left + right
+
+    def u_drain():
+        def one(s, carry):
+            @pl.when(s > t)
+            def _():
+                each_piece(lambda piece: u_hop(s, piece, 0).wait_send())
+
+            @pl.when(s < t)
+            def _():
+                each_piece(lambda piece: u_hop(s, piece, 1).wait_send())
+
+            return carry
+
+        lax.fori_loop(0, ring, one, 0)
 
     grad_keys = slope
     slots = [
@@ -655,7 +727,6 @@
         lambda: (up_sum.stage(2), down_sum.stage(3)),
         lambda: (up_sum.stage(3), down_sum.stage(4)),
     ]
-    step_done = 0
     for at in reversed(range(blocks)):
 
         def backward_head(head, carry, at=at):
@@ -718,12 +789,9 @@
             vectors[0:1, 0:width] += jnp.sum(grad_one * unit, axis=0, keepdims=True)
             vectors[1:2, 0:width] += jnp.sum(grad_one, axis=0, keepdims=True)
             u_all[at_rows, :] += grad_one * gain_one
-            grad_chain_step(step_done)
-            step_done += 1
+            u_start(s)
         if slots:
             slots.pop(0)()
-        if branch_hops:
-            branch_hop(branch_hops.pop(0))
 
     while slots:
         slots.pop(0)()
@@ -787,21 +855,20 @@
         spots, (part_mix, done2, half2, a12, b12, a22, b22), data_send.at[2], data_recv.at[2]
     )
     mix_sum.stage(0)
-    late = iter(range(ring, 3 * ring - 4))
-
-    def late_step(count=1):
-        for _, j in zip(range(count), late):
-            grad_chain_step(j)
+    last_tick = (PIECES + 2) * ring - 6
+
+    def ticks(share_from, share_to):
+        u_steps(last_tick * share_from // 18, last_tick * share_to // 18)
 
     up_sum.stage(4)
-    late_step()
+    ticks(0, 9)
     mix_sum.stage(1)
     down_sum.stage(5)
     finish_vec()
     finish_vec = vec_round(
         vec_core, ring, core, 2, lambda peer: dict(dp=dp_of(peer, x_at, y_at))
     )
-    late_step()
+    ticks(9, 12)
     up_sum.stage(5)
     mix_sum.stage(2)
     finish_vec()
@@ -811,7 +878,7 @@
     down_sum.stage(6)
     copies = [pltpu.make_async_copy(done0, grad_down_out, out_sem.at[0])]
     copies[-1].start()
-    late_step()
+    ticks(12, 15)
     mix_sum.stage(3)
     up_sum.stage(6)
     copies.append(pltpu.make_async_copy(done1, grad_up_out, out_sem.at[1]))
@@ -820,7 +887,7 @@
     finish_vec = vec_round(
         vec_y, ring + 2 + nx, y_at, 2, lambda peer: dict(dp=dp_of(core, x_at, peer))
     )
-    late_step(2 * ring)
+    ticks(15, 18)
     mix_sum.stage(4)
     branch_buf[t] = (x_all[rows(t), :].astype(full) + branch_own()).astype(low)
     copies.append(pltpu.make_async_copy(branch_buf.at[t], output_rows, out_sem.at[2]))
@@ -836,7 +903,7 @@
     vectors_out[4:5, :] = jnp.broadcast_to(rms_context, (1, vectors.shape[1]))
     vectors_out[5:6, :] = jnp.broadcast_to(rms_active, (1, vectors.shape[1]))
     vectors_out[6:8, :] = jnp.zeros_like(vectors_out[6:8, :])
-    weighted = grad_own()
+    weighted = u_own()
     own_load.wait()
     unit, scale = unit_rows(x_all[rows(t), :].astype(full))
     grad_rows = scale * (
@@ -868,7 +935,7 @@
         copies[-1].start()
     gather_drain(0)
     branch_drain()
-    grad_drain()
+    u_drain()
     for copy in copies:
         copy.wait()
 
@@ -972,7 +1039,7 @@
             wider(group, LANES), wider(group, LANES),
             sems(2, 2, ring), sems(2, ring),
             scratch(ring + 1, shard, width), sems(ring), sems(ring + 1),
-            scratch(ring + 1, shard, width), sems(ring), sems(ring + 1),
+            scratch(ring + 1, shard, width), sems(ring, PIECES), sems(ring + 1, PIECES),
             *sum_buffers(hidden_local, width),
             *sum_buffers(width, hidden_local)[1:],
             *sum_buffers(width, 4 * local)[1:],

time: 176 us -> 174 us (0.989)
  Pallas kernels: 175 us -> 173 us
    pallas_call x1, Pallas kernels: 166 us -> 164 us  [per_device(): pl.pallas_call(partial(layer_kernel, ring, ranks), name='layer', out_shap...]
where the time goes in v3:
time: 174 us
  Pallas kernels  173 us (99%)
    pallas_call x1, Pallas kernels, per_device(): pl.pallas_call(partial(layer_kernel, ring, ranks), name='layer', out_shap...  164 us
    pallas_call x1, Pallas kernels, widen(): pl.pallas_call(widen_kernel, name='widen', grid=(steps,), out_shape=[jax....  9.18 us

profile of v3, /device:TPU:0, one launch (start us, length us, event | category | flops | bytes accessed | tf_op | source)
XLA Modules:
  0.0 173.5 jit_solution(12998285105836876659)
XLA Ops:
  0.6 163.5 %layer.1 = (bf16[256,1024]{1,0:T(8,128)(2,1)}, bf16[256,1024]{1,0:T(8,128)(2,1)}, bf16[1024,1024]{1,0:T(8,128)(2,1)}, bf16[1024,1024]{1,0:T(8,128)(2,1)}, bf16[3...) custom-call(bf16[256,1024]{1,0:T(8,128)(2,1)} %tokens.1, bf16[256,1024]{1,0:T(8,128)(2,1)} %cotangent.1, ...), custom_call_target="tpu_custom_call" | custom-call | tf_op jit(solution)/shard_map/layer/pallas_call | solution.py:1011
  164.2 9.2 %widen.1 = (bf16[256,1024]{1,0:T(8,128)(2,1)}, bf16[256,1024]{1,0:T(8,128)(2,1)}, f32[1024,1024]{1,0:T(8,128)}, f32[1024,1024]{1,0:T(8,128)}, f32[3,1024,256]{2,...) custom-call(bf16[256,1024]{1,0:T(8,128)(2,1)} %get-tuple-element.31., ...), custom_call_target="tpu_custom_call" | custom-call | tf_op jit(solution)/shard_map/widen/pallas_call | solution.py:964

commit v4 on v3

--- a/solution.py
+++ b/solution.py
@@ -14,7 +14,7 @@
 BLOCK = 256
 LONGEST = 512
 LANES = 128
-PIECES = 1
+PIECES = 2
 
 epsilon = 1e-05
 rotary_base = 10000.0
@@ -861,14 +861,14 @@
         u_steps(last_tick * share_from // 18, last_tick * share_to // 18)
 
     up_sum.stage(4)
-    ticks(0, 9)
+    ticks(0, 11)
     mix_sum.stage(1)
     down_sum.stage(5)
     finish_vec()
     finish_vec = vec_round(
         vec_core, ring, core, 2, lambda peer: dict(dp=dp_of(peer, x_at, y_at))
     )
-    ticks(9, 12)
+    ticks(11, 15)
     up_sum.stage(5)
     mix_sum.stage(2)
     finish_vec()
@@ -878,7 +878,7 @@
     down_sum.stage(6)
     copies = [pltpu.make_async_copy(done0, grad_down_out, out_sem.at[0])]
     copies[-1].start()
-    ticks(12, 15)
+    ticks(15, 18)
     mix_sum.stage(3)
     up_sum.stage(6)
     copies.append(pltpu.make_async_copy(done1, grad_up_out, out_sem.at[1]))
@@ -887,7 +887,6 @@
     finish_vec = vec_round(
         vec_y, ring + 2 + nx, y_at, 2, lambda peer: dict(dp=dp_of(core, x_at, peer))
     )
-    ticks(15, 18)
     mix_sum.stage(4)
     branch_buf[t] = (x_all[rows(t), :].astype(full) + branch_own()).astype(low)
     copies.append(pltpu.make_async_copy(branch_buf.at[t], output_rows, out_sem.at[2]))
@@ -950,7 +949,7 @@
 
 
 def widen(arrays, vectors, width):
-    steps = 8
+    steps = 4
 
     def spec(shape):
         block = list(shape)

time: 174 us -> 169 us (0.971)
  Pallas kernels: 173 us -> 167 us
    pallas_call x1, Pallas kernels: 164 us -> 159 us  [per_device(): pl.pallas_call(partial(layer_kernel, ring, ranks), name='layer', out_shap...]
where the time goes in v4:
time: 169 us; the launch traced here: 168 us
  Pallas kernels  167 us (99%)
    pallas_call x1, Pallas kernels, per_device(): pl.pallas_call(partial(layer_kernel, ring, ranks), name='layer', out_shap...  159 us
    pallas_call x1, Pallas kernels, widen(): pl.pallas_call(widen_kernel, name='widen', grid=(steps,), out_shape=[jax....  8.43 us

profile of v4, /device:TPU:0, one launch (start us, length us, event | category | flops | bytes accessed | tf_op | source)
XLA Modules:
  0.0 168.0 jit_solution(4867210975557265700)
XLA Ops:
  0.6 158.7 %layer.1 = (bf16[256,1024]{1,0:T(8,128)(2,1)}, bf16[256,1024]{1,0:T(8,128)(2,1)}, bf16[1024,1024]{1,0:T(8,128)(2,1)}, bf16[1024,1024]{1,0:T(8,128)(2,1)}, bf16[3...) custom-call(bf16[256,1024]{1,0:T(8,128)(2,1)} %tokens.1, bf16[256,1024]{1,0:T(8,128)(2,1)} %cotangent.1, ...), custom_call_target="tpu_custom_call" | custom-call | tf_op jit(solution)/shard_map/layer/pallas_call | solution.py:1010
  159.4 8.4 %widen.1 = (bf16[256,1024]{1,0:T(8,128)(2,1)}, bf16[256,1024]{1,0:T(8,128)(2,1)}, f32[1024,1024]{1,0:T(8,128)}, f32[1024,1024]{1,0:T(8,128)}, f32[3,1024,256]{2,...) custom-call(bf16[256,1024]{1,0:T(8,128)(2,1)} %get-tuple-element.31., ...), custom_call_target="tpu_custom_call" | custom-call | tf_op jit(solution)/shard_map/widen/pallas_call | solution.py:963
